TPU v7x, 32 devices: a whole 2x2x4 slice. The times are simulated.
32 devices in a mesh: dp: 2 (over x), tx: 4 (over z), tyz: 4 (over y, core).
Axes of the slice: x: 2, y: 2, z: 4, core: 2. Of those that a mesh axis runs over, the one named last changes fastest.
Arguments:
- residual: bfloat16 [2048, 2560], P('dp', ('tx', 'tyz')), parts along dimension 0
- ln_scale: bfloat16 [2560], P(('tx', 'tyz'))
- w_query: bfloat16 [2560, 2560], P('tx', 'tyz')
- w_key: bfloat16 [2560, 80], P('tx')
- w_value: bfloat16 [2560, 80], P('tx')
- w_gate: bfloat16 [2560, 10240], P('tx', 'tyz')
- w_up: bfloat16 [2560, 10240], P('tx', 'tyz')
- w_out: bfloat16 [2560, 2560], P('tyz', 'tx')
- w_down: bfloat16 [10240, 2560], P('tyz', 'tx')
- k_cache: bfloat16 [2048, 1024, 80], P(('dp', 'tx', 'tyz')), parts along dimension 0
- v_cache: bfloat16 [2048, 1024, 80], P(('dp', 'tx', 'tyz')), parts along dimension 0
- lengths: int32 [2048], P(('dp', 'tx', 'tyz')), parts along dimension 0
Outputs:
- output 1: bfloat16 [2048, 2560], P('dp', ('tx', 'tyz')), parts along dimension 0
- output 2: bfloat16 [2048, 1024, 80], P(('dp', 'tx', 'tyz')), parts along dimension 0
- output 3: bfloat16 [2048, 1024, 80], P(('dp', 'tx', 'tyz')), parts along dimension 0
There are 2 independent parts. A program takes and returns all parts, laid end to end along the dimension named above; an argument that names none is the same for every part.
All inputs are finite; a program needn't handle non-finite values.
Results may differ from a plain program's by a relative error of at most 0.0155287.
Values are sent between devices in bfloat16 or wider.
A program may use at most 1 GiB of HBM per device.

v0:
```python
import jax
import jax.numpy as jnp
from jax import lax
from jax.sharding import PartitionSpec as P

LN_EPS = 1e-5
ROPE_BASE = 10000.0


def rope_rotate(vectors, positions):
    head_dim = vectors.shape[-1]
    half_dim = head_dim // 2
    inv_freq = ROPE_BASE ** (-2.0 * jnp.arange(half_dim, dtype=jnp.float32) / head_dim)
    angles = positions.astype(jnp.float32)[:, None] * inv_freq[None, :]
    bcast_shape = (angles.shape[0],) + (1,) * (vectors.ndim - 2) + (half_dim,)
    cos_part = jnp.cos(angles).reshape(bcast_shape)
    sin_part = jnp.sin(angles).reshape(bcast_shape)
    vec_f32 = vectors.astype(jnp.float32)
    first_half = vec_f32[..., :half_dim]
    second_half = vec_f32[..., half_dim:]
    rotated = jnp.concatenate([first_half * cos_part - second_half * sin_part, second_half * cos_part + first_half * sin_part], axis=-1)
    return rotated.astype(jnp.bfloat16)


def attend_rows(query_rot, key_rot, value_new, k_cache, v_cache, lengths):
    positions = jnp.arange(k_cache.shape[1], dtype=jnp.int32)
    write_mask = (positions[None, :] == lengths[:, None])[:, :, None]
    k_updated = jnp.where(write_mask, key_rot[:, None, :], k_cache)
    v_updated = jnp.where(write_mask, value_new[:, None, :], v_cache)
    scores = jnp.einsum('rhd,rtd->rht', query_rot, k_updated, preferred_element_type=jnp.float32) * (query_rot.shape[-1] ** -0.5)
    valid_mask = (positions[None, :] <= lengths[:, None])[:, None, :]
    scores = jnp.where(valid_mask, scores, -1e30)
    attn_probs = jax.nn.softmax(scores, axis=-1).astype(jnp.bfloat16)
    attended = jnp.einsum('rht,rtd->rhd', attn_probs, v_updated, preferred_element_type=jnp.float32).astype(jnp.bfloat16)
    return attended, k_updated, v_updated


def solution(mesh):
    tx_size = mesh.shape['tx']
    tyz_size = mesh.shape['tyz']
    row_axes = ('dp', 'tx', 'tyz')

    def decode_layer(residual, ln_scale, w_query, w_key, w_value, w_gate, w_up, w_out, w_down, k_cache, v_cache, lengths):
        model_dim = residual.shape[1] * tx_size * tyz_size
        rows_local = k_cache.shape[0]
        head_dim = w_key.shape[1]
        res_f32 = residual.astype(jnp.float32)
        row_stats = jnp.stack([jnp.sum(res_f32, axis=1), jnp.sum(jnp.square(res_f32), axis=1)])
        row_stats = lax.psum(row_stats, ('tx', 'tyz'))
        row_mean = row_stats[0] / model_dim
        row_var = row_stats[1] / model_dim - jnp.square(row_mean)
        normed = ((res_f32 - row_mean[:, None]) * lax.rsqrt(row_var + LN_EPS)[:, None] * ln_scale.astype(jnp.float32)).astype(jnp.bfloat16)
        normed_tx = lax.all_gather(normed, 'tyz', axis=1, tiled=True)
        gate_part = jnp.dot(normed_tx, w_gate, preferred_element_type=jnp.float32).astype(jnp.bfloat16)
        up_part = jnp.dot(normed_tx, w_up, preferred_element_type=jnp.float32).astype(jnp.bfloat16)
        query_part = jnp.dot(normed_tx, w_query, preferred_element_type=jnp.float32).astype(jnp.bfloat16)
        key_part = jnp.dot(normed_tx, w_key, preferred_element_type=jnp.float32).astype(jnp.bfloat16)
        value_part = jnp.dot(normed_tx, w_value, preferred_element_type=jnp.float32).astype(jnp.bfloat16)
        gate_sum = lax.psum_scatter(gate_part, 'tx', scatter_dimension=1, tiled=True)
        up_sum = lax.psum_scatter(up_part, 'tx', scatter_dimension=1, tiled=True)
        mlp_act = (jax.nn.silu(gate_sum.astype(jnp.float32)) * up_sum.astype(jnp.float32)).astype(jnp.bfloat16)
        act_full = lax.all_gather(mlp_act, 'tx', axis=1, tiled=True)
        query_rows = lax.psum_scatter(query_part, 'tx', scatter_dimension=0, tiled=True)
        key_rows = lax.psum_scatter(key_part, 'tx', scatter_dimension=0, tiled=True)
        value_rows = lax.psum_scatter(value_part, 'tx', scatter_dimension=0, tiled=True)
        query_mine = lax.all_to_all(query_rows.reshape(query_rows.shape[0], -1, head_dim), 'tyz', 0, 1, tiled=True)
        row_start = lax.axis_index('tyz') * rows_local
        key_mine = lax.dynamic_slice_in_dim(key_rows, row_start, rows_local, axis=0)
        value_mine = lax.dynamic_slice_in_dim(value_rows, row_start, rows_local, axis=0)
        query_rot = rope_rotate(query_mine, lengths)
        key_rot = rope_rotate(key_mine, lengths)
        attended, k_updated, v_updated = attend_rows(query_rot, key_rot, value_mine, k_cache, v_cache, lengths)
        attended_heads = lax.all_to_all(attended, 'tyz', 1, 0, tiled=True)
        attended_all = lax.all_gather(attended_heads, 'tx', axis=0, tiled=True)
        attended_flat = attended_all.reshape(attended_all.shape[0], -1)
        block_part = jnp.dot(attended_flat, w_out, preferred_element_type=jnp.float32) + jnp.dot(act_full, w_down, preferred_element_type=jnp.float32)
        block_sum = lax.psum_scatter(block_part.astype(jnp.bfloat16), 'tyz', scatter_dimension=1, tiled=True)
        new_resid = (res_f32 + block_sum.astype(jnp.float32)).astype(jnp.bfloat16)
        return new_resid, k_updated, v_updated

    in_specs = (P('dp', ('tx', 'tyz')), P(('tx', 'tyz')), P('tx', 'tyz'), P('tx', None), P('tx', None), P('tx', 'tyz'), P('tx', 'tyz'), P('tyz', 'tx'), P('tyz', 'tx'), P(row_axes, None, None), P(row_axes, None, None), P(row_axes))
    out_specs = (P('dp', ('tx', 'tyz')), P(row_axes, None, None), P(row_axes, None, None))
    return jax.shard_map(decode_layer, mesh=mesh, in_specs=in_specs, out_specs=out_specs, check_vma=False)
```

profile of v0, /device:TPU:0, one launch (start us, length us, event | category | flops | bytes accessed | tf_op | source)
XLA Modules:
  0.0 513.8 jit_solution(11486656006953824679)
XLA Ops:
  8.5 35.5 %psum.7 = f32[2,1024]{1,0:T(2,128)S(1)} all-reduce(f32[2,1024]{1,0:T(2,128)S(1)} %pad_maximum_fusion.1), channel_id=1, replica_groups=mesh['dp'=2,'tx'=4,'tyz'=4] {'tx','tyz'}, use_global_device_ids=true, to_apply=%region_2.0 | all-reduce | flops 2048 | bytes 16384 | tf_op jit(solution)/shard_map/psum | solution.py:49
  46.6 15.3 %all-gather.4.cloned.1.call-done = bf16[1024,640]{0,1:T(8,128)(2,1)} async-done(((bf16[1024,160]{0,1:T(8,128)(2,1)}), bf16[1024,640]{0,1:T(8,128)(2,1)}) %all-gather.4.cloned.1.call-update) | async-done | bytes 1310736 | tf_op jit(solution)/shard_map/all_gather | solution.py:53
  61.9 7.3 %convolution_convert_fusion.1 = bf16[1024,2560]{1,0:T(8,128)(2,1)} fusion(bf16[1024,640]{0,1:T(8,128)(2,1)} %all-gather.4.cloned.1.call-done, bf16[640,2560]{1,0:T(8,128)(2,1)S(1)} %copy-done), kind=kOutput, calls=%fused_computation.8 | convolution fusion | flops 3358064640 | bytes 9830400 | tf_op jit(solution)/shard_map/dot_general | solution.py:54
  69.2 7.9 %copy.47 = bf16[1024,2560]{0,1:T(8,128)(2,1)} copy(bf16[1024,2560]{1,0:T(8,128)(2,1)} %convolution_convert_fusion.1) | data formatting | bytes 10485760
  78.5 7.9 %convolution_convert_fusion = bf16[1024,2560]{1,0:T(8,128)(2,1)} fusion(bf16[1024,640]{0,1:T(8,128)(2,1)S(1)} %copy-done.2, bf16[640,2560]{1,0:T(8,128)(2,1)} %param.18), kind=kOutput, calls=%fused_computation.7 | convolution fusion | flops 3358064640 | bytes 9830400 | tf_op jit(solution)/shard_map/dot_general | solution.py:55
  86.4 7.9 %copy.49 = bf16[1024,2560]{0,1:T(8,128)(2,1)} copy(bf16[1024,2560]{1,0:T(8,128)(2,1)} %convolution_convert_fusion) | data formatting | bytes 10485760
  97.5 2.4 convolution_convert_fusion.2
  100.0 70.9 %reduce-scatter.19.cloned.1.call-done = bf16[640,1024]{1,0:T(8,128)(2,1)} async-done(((bf16[2560,1024]{1,0:T(8,128)(2,1)}), bf16[640,1024]{1,0:T(8,128)(2,1)}) %reduce-scatter.19.cloned.1.call-update) | async-done | bytes 1310736
  172.6 95.5 %reduce-scatter.21.cloned.1.call-done = bf16[640,1024]{1,0:T(8,128)(2,1)} async-done(((bf16[2560,1024]{1,0:T(8,128)(2,1)}), bf16[640,1024]{1,0:T(8,128)(2,1)}) %reduce-scatter.21.cloned.1.call-update) | async-done | bytes 1310736
  269.8 1.9 fusion.10
  271.9 19.0 %reduce-scatter.13.cloned.1.call-done = bf16[256,80]{0,1:T(8,128)(2,1)} async-done(((bf16[1024,80]{0,1:T(8,128)(2,1)}), bf16[256,80]{0,1:T(8,128)(2,1)}) %reduce-scatter.13.cloned.1.call-update) | async-done | bytes 40976 | tf_op jit(solution)/shard_map/reduce_scatter | solution.py:64
  290.9 19.7 %reduce-scatter.15.cloned.1.call-done = bf16[256,80]{0,1:T(8,128)(2,1)} async-done(((bf16[1024,80]{0,1:T(8,128)(2,1)}), bf16[256,80]{0,1:T(8,128)(2,1)}) %reduce-scatter.15.cloned.1.call-update) | async-done | bytes 40976 | tf_op jit(solution)/shard_map/reduce_scatter | solution.py:65
  311.9 31.3 %reduce-scatter.11.cloned.1.call-done = bf16[256,640]{1,0:T(8,128)(2,1)} async-done(((bf16[1024,640]{1,0:T(8,128)(2,1)}), bf16[256,640]{1,0:T(8,128)(2,1)}) %reduce-scatter.11.cloned.1.call-update) | async-done | bytes 327696 | tf_op jit(solution)/shard_map/reduce_scatter | solution.py:63
  345.4 3.5 all-to-all-start
  349.1 16.3 %broadcast_select_fusion.1 = (bf16[64,1024,80]{1,2,0:T(8,128)(2,1)}, bf16[64,1024,80]{1,2,0:T(8,128)(2,1)}) fusion(bf16[64,1024,80]{1,2,0:T(8,128)(2,1)} %param.21, pred[64,1024]{1,0:T(8,128)(4,1)S(1)} %get-tuple-element.18, bf16[64,80]{1,0:T(8,128)(2,1)S(1)} %copy.42, bf16[64,1024,80]{1,2,0:T(8,128)(2,1)} %param.22, bf16[64,80]{1,0:T(8,128)(2,1)S(1)} %copy.43), kind=kLoop, calls=%fused_computation.2 | loop fusion | flops 10485760 | bytes 42029056 | tf_op jit(solution)/shard_map/jit(_where)/select_n | solution.py:28
  366.2 5.0 fusion.17
  371.2 5.2 %fusion.24 = (f32[64,32]{1,0:T(8,128)S(1)}, f32[64,32,1024]{2,1,0:T(8,128)}) fusion(f32[64,32,1024]{2,1,0:T(8,128)S(1)} %fusion.17, pred[64,1024]{1,0:T(8,128)(4,1)S(1)} %get-tuple-element.17), kind=kOutput, calls=%fused_computation.59 | output fusion | flops 12583935 | bytes 16850944 | tf_op jit(solution)/shard_map/sub | solution.py:33
  376.4 9.4 %fusion.11 = bf16[64,32,80]{2,1,0:T(8,128)(2,1)S(1)} fusion(bf16[64,1024,80]{1,2,0:T(8,128)(2,1)} %get-tuple-element.8, f32[64,32,1024]{2,1,0:T(8,128)} %get-tuple-element.20, f32[64,32]{1,0:T(8,128)S(1)} %get-tuple-element.19), kind=kOutput, calls=%fused_computation.22 | convolution fusion | flops 339902464 | bytes 19210240 | tf_op jit(solution)/shard_map/rht,rtd->rhd/dot_general | solution.py:34
  386.0 11.6 %all_to_all.27 = bf16[64,32,80]{2,0,1:T(8,128)(2,1)S(1)} all-to-all(bf16[64,32,80]{2,0,1:T(8,128)(2,1)S(1)} %copy.44), channel_id=1, replica_groups=mesh['dp'=2,'tx'=4,'tyz'=4] {'tyz'}, dimensions={1} | all-to-all | bytes 655360 | tf_op jit(solution)/shard_map/all_to_all | solution.py:73
  399.1 41.7 %all-gather.8.cloned.1.call-done = bf16[1024,2560]{1,0:T(8,128)(2,1)} async-done(((bf16[1024,640]{1,0:T(8,128)(2,1)}), bf16[1024,2560]{1,0:T(8,128)(2,1)}) %all-gather.8.cloned.1.call-update) | async-done | bytes 5242896 | tf_op jit(solution)/shard_map/all_gather | solution.py:62
  440.8 8.7 %fusion.25 = f32[1024,640]{0,1:T(8,128)} fusion(bf16[1024,2560]{1,0:T(8,128)(2,1)} %all-gather.8.cloned.1.call-done, bf16[2560,640]{1,0:T(8,128)(2,1)} %param.20), kind=kOutput, calls=%fused_computation.60 | convolution fusion | flops 3355443200 | bytes 11141120 | tf_op jit(solution)/shard_map/dot_general | solution.py:76
  449.5 26.6 %all-gather.6.cloned.1.call-done = bf16[1024,8,80]{0,2,1:T(8,128)(2,1)} async-done(((bf16[256,8,80]{0,2,1:T(8,128)(2,1)}), bf16[1024,8,80]{0,2,1:T(8,128)(2,1)}) %all-gather.6.cloned.1.call-update) | async-done | bytes 1310736 | tf_op jit(solution)/shard_map/all_gather | solution.py:74
  476.1 4.9 add_convert_fusion
  481.0 24.3 %reduce-scatter.17.cloned.1.call-done = bf16[1024,160]{0,1:T(8,128)(2,1)} async-done(((bf16[1024,640]{0,1:T(8,128)(2,1)}), bf16[1024,160]{0,1:T(8,128)(2,1)}) %reduce-scatter.17.cloned.1.call-update) | async-done | bytes 327696 | tf_op jit(solution)/shard_map/reduce_scatter | solution.py:77
  (61 shorter events, 19.8 us)
Async XLA Ops:
  7.2 54.7 %copy-start = (bf16[640,2560]{1,0:T(8,128)(2,1)S(1)}, bf16[640,2560]{1,0:T(8,128)(2,1)}, u32[]{:S(2)}) copy-start(bf16[640,2560]{1,0:T(8,128)(2,1)} %param.17) | copy-start | bytes 9830404
  7.2 54.7 %all-gather.4.cloned.1.call-start = ((), (), s32[]{:S(2)}) async-start(), calls=%async_computation.8 | async-start | bytes 1638400 | tf_op jit(solution)/shard_map/all_gather | solution.py:53
  46.5 124.4 %reduce-scatter.19.cloned.1.call-start = ((), (), s32[]{:S(2)}) async-start(), calls=%async_computation.15 | async-start | bytes 6553600
  77.2 1.3 copy-start.2
  77.2 190.9 %reduce-scatter.21.cloned.1.call-start = ((), (), s32[]{:S(2)}) async-start(), calls=%async_computation.16 | async-start | bytes 6553600
  94.3 0.9 copy-start.3
  94.3 2.0 copy-start.4
  94.3 3.1 copy-start.6
  94.4 196.5 %reduce-scatter.13.cloned.1.call-start = ((), (), s32[]{:S(2)}) async-start(), calls=%async_computation.10 | async-start | bytes 204800 | tf_op jit(solution)/shard_map/reduce_scatter | solution.py:64
  96.3 214.4 %reduce-scatter.15.cloned.1.call-start = ((), (), s32[]{:S(2)}) async-start(), calls=%async_computation.11 | async-start | bytes 204800 | tf_op jit(solution)/shard_map/reduce_scatter | solution.py:65
  97.4 245.7 %reduce-scatter.11.cloned.1.call-start = ((), (), s32[]{:S(2)}) async-start(), calls=%async_computation.9 | async-start | bytes 1638400 | tf_op jit(solution)/shard_map/reduce_scatter | solution.py:63
  99.9 340.9 %all-gather.8.cloned.1.call-start = ((), (), s32[]{:S(2)}) async-start(), calls=%async_computation.13 | async-start | bytes 6553600 | tf_op jit(solution)/shard_map/all_gather | solution.py:62
  269.8 1.9 copy-start.5
  345.4 20.2 %all-to-all-start = ((bf16[256,8,80]{2,1,0:T(8,128)(2,1)}), bf16[256,8,80]{2,1,0:T(8,128)(2,1)S(1)}, u32[]{:S(2)}, u32[]{:S(2)}) async-start(bf16[256,8,80]{2,1,0:T(8,128)(2,1)} %copy.38), calls=%async_computation.1 | async-start | bytes 1048576 | tf_op jit(solution)/shard_map/all_to_all | solution.py:66
  348.8 127.3 %all-gather.6.cloned.1.call-start = ((), (), s32[]{:S(2)}) async-start(), calls=%async_computation.12 | async-start | bytes 1638400 | tf_op jit(solution)/shard_map/all_gather | solution.py:74
  399.1 106.3 %reduce-scatter.17.cloned.1.call-start = ((), (), s32[]{:S(2)}) async-start(), calls=%async_computation.14 | async-start | bytes 1638400 | tf_op jit(solution)/shard_map/reduce_scatter | solution.py:77
  476.1 31.1 %copy-start.1 = (bf16[640,2560]{1,0:T(8,128)(2,1)S(1)}, bf16[640,2560]{1,0:T(8,128)(2,1)}, u32[]{:S(2)}) copy-start(bf16[640,2560]{1,0:T(8,128)(2,1)} %param.17) | copy-start | bytes 9830404
Sparse Core Ops, SparseCore 0:
  46.6 15.2 all-gather.3
  77.3 93.5 reduce-scatter.18
  173.8 94.2 reduce-scatter.20
  270.8 20.1 reduce-scatter.12
  293.0 17.6 reduce-scatter.14
  313.4 29.6 reduce-scatter.10
  344.7 96.0 all-gather.7
  443.0 33.0 all-gather.5
  481.1 24.1 reduce-scatter.16
where the time goes:
time: 515 us; the launch traced here: 514 us
  waiting for transfers between devices  345 us (67%)
  matrix products  47.7 us (9%)
  blocking collectives  47.1 us (9%)
  other arithmetic  30.8 us (6%)
  local copies, waits for them, and re-layouts  25.6 us (5%)
  between operations  14 us (3%)
    unnamed x11, waiting for transfers between devices  167 us
    all_gather x1, waiting for transfers between devices, decode_layer(): act_full = lax.all_gather(mlp_act, 'tx', axis=1, tiled=True)  41.7 us
    psum x1, blocking collectives, decode_layer(): row_stats = lax.psum(row_stats, ('tx', 'tyz'))  35.5 us
    reduce_scatter x1, waiting for transfers between devices, decode_layer(): lax.psum_scatter(query_part, 'tx', scatter_dimension=0, tiled=True)  31.3 us
    all_gather x1, waiting for transfers between devices, decode_layer(): attended_all = lax.all_gather(attended_heads, 'tx', axis=0, tiled=True)  26.6 us
    reduce_scatter x1, waiting for transfers between devices, decode_layer(): lax.psum_scatter(block_part.astype(jnp.bfloat16), 'tyz', scatter_dimensio...  24.3 us
    unnamed x18, local copies, waits for them, and re-layouts  21.4 us
    reduce_scatter x1, waiting for transfers between devices, decode_layer(): lax.psum_scatter(value_part, 'tx', scatter_dimension=0, tiled=True)  19.7 us
  transfers between devices with their start and end apart: 10, of which 9 were waited for; matrix products, arithmetic and copies ran while one was open for 15% of the time, Pallas kernels for 0%

commit v1 on v0

v1 whole, which is shorter than its diff:
```python
import functools

import jax
import jax.numpy as jnp
from jax import lax
from jax.experimental import pallas as pl
from jax.experimental.pallas import tpu as pltpu
from jax.sharding import PartitionSpec as P

LN_EPS = 1e-5
ROPE_BASE = 10000.0
MESH = pl.DeviceIdType.MESH
NZ = 4
EXTRA = 16


def position():
    dp = lax.axis_index("dp")
    z = lax.axis_index("tx")
    ty = lax.axis_index("tyz")
    return dp, z, ty // 2, ty % 2


def neighbour_barrier(dp, z, y, c):
    sem = pltpu.get_barrier_semaphore()

    def greet(device):
        pl.semaphore_signal(sem, inc=1, device_id=device, device_id_type=MESH)

    pl.when(z > 0)(lambda: greet((dp, z - 1, y * 2 + c)))
    pl.when(z < NZ - 1)(lambda: greet((dp, z + 1, y * 2 + c)))
    greet((dp, z, (1 - y) * 2 + c))
    greet((dp, z, y * 2 + 1 - c))
    inner = jnp.logical_and(z > 0, z < NZ - 1)
    pl.when(inner)(lambda: pl.semaphore_wait(sem, 4))
    pl.when(jnp.logical_not(inner))(lambda: pl.semaphore_wait(sem, 3))


def gather_kernel(x_ref, out_ref, lsem, zs, zr, ys, yr, cs, cr):
    dp, z, y, c = position()
    ty = y * 2 + c
    peer_y, peer_c = (1 - y) * 2 + c, y * 2 + 1 - c
    local = pltpu.make_async_copy(x_ref, out_ref.at[0, ty], lsem)
    local.start()
    neighbour_barrier(dp, z, y, c)
    local.wait()

    def z_copy(o, step):
        slot = lax.rem(o + step + NZ, NZ)
        return pltpu.make_async_remote_copy(
            out_ref.at[o, ty], out_ref.at[slot, ty],
            zs.at[o, (step + 1) // 2], zr.at[slot], device_id=(dp, z + step, ty), device_id_type=MESH)

    def z_arrived(o):
        return pltpu.make_async_remote_copy(
            out_ref.at[o, ty], out_ref.at[o, ty], zs.at[o, 0], zr.at[o],
            device_id=(dp, z, peer_y), device_id_type=MESH)

    def y_copy(o):
        return pltpu.make_async_remote_copy(
            out_ref.at[o, ty], out_ref.at[o, ty], ys.at[o], yr.at[o],
            device_id=(dp, z, peer_y), device_id_type=MESH)

    def y_arrived(o):
        return pltpu.make_async_remote_copy(
            out_ref.at[o, peer_y], out_ref.at[o, peer_y], ys.at[o], yr.at[o],
            device_id=(dp, z, peer_y), device_id_type=MESH)

    def c_copy(o, yy):
        return pltpu.make_async_remote_copy(
            out_ref.at[o, yy * 2 + c], out_ref.at[o, yy * 2 + c], cs.at[o, yy], cr.at[o, yy],
            device_id=(dp, z, peer_c), device_id_type=MESH)

    def c_arrived(o, yy):
        return pltpu.make_async_remote_copy(
            out_ref.at[o, yy * 2 + 1 - c], out_ref.at[o, yy * 2 + 1 - c], cs.at[o, yy], cr.at[o, yy],
            device_id=(dp, z, peer_c), device_id_type=MESH)

    pl.when(z < NZ - 1)(lambda: z_copy(0, 1).start())
    pl.when(z > 0)(lambda: z_copy(0, -1).start())
    y_copy(0).start()
    c_copy(0, y).start()
    for d in range(1, NZ):
        for o, here, onward, step in (
                (d, z >= d, z < NZ - 1, 1), (NZ - d, z + d < NZ, z > 0, -1)):
            def handle(o=o, onward=onward, step=step):
                z_arrived(o).wait_recv()
                pl.when(onward)(lambda: z_copy(o, step).start())
                y_copy(o).start()
                c_copy(o, y).start()
            pl.when(here)(handle)
    for d in range(NZ):
        for o, here in ((d, z >= d), (NZ - d, z + d < NZ)):
            if d == 0 and o == NZ:
                continue

            def handle(o=o):
                y_arrived(o).wait_recv()
                c_copy(o, 1 - y).start()
            pl.when(here)(handle)
    for o in range(NZ):
        y_copy(o).wait_send()
        for yy in range(2):
            c_copy(o, yy).wait_send()
            c_arrived(o, yy).wait_recv()
    pl.when(z < NZ - 1)(lambda: z_copy(0, 1).wait_send())
    pl.when(z > 0)(lambda: z_copy(0, -1).wait_send())
    for d in range(1, NZ):
        pl.when(jnp.logical_and(z >= d, z < NZ - 1))(lambda d=d: z_copy(d, 1).wait_send())
        pl.when(jnp.logical_and(z + d < NZ, z > 0))(lambda d=d: z_copy(NZ - d, -1).wait_send())


def gather_blocks(block):
    rows, lanes = block.shape
    dma = pltpu.SemaphoreType.DMA
    return pl.pallas_call(
        gather_kernel,
        out_shape=jax.ShapeDtypeStruct((NZ, 4, rows, lanes), block.dtype),
        in_specs=[pl.BlockSpec(memory_space=pl.ANY)],
        out_specs=pl.BlockSpec(memory_space=pltpu.VMEM),
        scratch_shapes=[dma, dma((NZ, 2)), dma((NZ,)), dma((NZ,)), dma((NZ,)), dma((NZ, 2)), dma((NZ, 2))],
        compiler_params=pltpu.CompilerParams(collective_id=0, has_side_effects=True,
                                             vmem_limit_bytes=12 * 2**20),
        name="gather_blocks",
    )(block)


def reduce_kernel(p_ref, res_ref, out_ref, cbuf, ysend, yrecv, zsend, zrecv, cs, cr, ys, yr, zs, zr):
    dp, z, y, c = position()
    ty = y * 2 + c
    peer_y, peer_c = (1 - y) * 2 + c, y * 2 + 1 - c
    neighbour_barrier(dp, z, y, c)

    def c_copy(o, yy):
        return pltpu.make_async_remote_copy(
            p_ref.at[o, yy * 2 + 1 - c], cbuf.at[o, yy], cs.at[o, yy], cr.at[o, yy],
            device_id=(dp, z, peer_c), device_id_type=MESH)

    def y_copy(o):
        return pltpu.make_async_remote_copy(
            ysend.at[o], yrecv.at[o], ys.at[o], yr.at[o],
            device_id=(dp, z, peer_y), device_id_type=MESH)

    def z_copy(o, step):
        slot = lax.rem(o + step + NZ, NZ)
        side = (1 - step) // 2
        return pltpu.make_async_remote_copy(
            zsend.at[o], zrecv.at[side, slot], zs.at[o], zr.at[side, slot],
            device_id=(dp, z + step, ty), device_id_type=MESH)

    def z_arrived(o, side):
        return pltpu.make_async_remote_copy(
            zsend.at[o], zrecv.at[side, o], zs.at[o], zr.at[side, o],
            device_id=(dp, z, peer_y), device_id_type=MESH)

    order = []
    for d in range(NZ - 1, 0, -1):
        order += [(NZ - d, z + d < NZ, 1), (d, z >= d, -1)]

    for yy in (1 - y, y):
        for o, here, _ in order:
            pl.when(here)(lambda o=o, yy=yy: c_copy(o, yy).start())
        c_copy(0, yy).start()

    def to_y(o):
        c_copy(o, 1 - y).wait_recv()
        ysend[o] = (p_ref[o, peer_y].astype(jnp.float32)
                    + cbuf[o, 1 - y].astype(jnp.float32)).astype(jnp.bfloat16)
        y_copy(o).start()

    for o, here, _ in order:
        pl.when(here)(functools.partial(to_y, o))
    to_y(0)

    def chip_pair_sum(o):
        c_copy(o, y).wait_recv()
        y_copy(o).wait_recv()
        return (p_ref[o, ty].astype(jnp.float32) + cbuf[o, y].astype(jnp.float32)
                + yrecv[o].astype(jnp.float32))

    def to_z(o, step):
        total = chip_pair_sum(o)
        side = (1 - step) // 2
        more = z > 0 if step == 1 else z < NZ - 1

        @pl.when(more)
        def _():
            z_arrived(o, side).wait_recv()
            zsend[o] = (total + zrecv[side, o].astype(jnp.float32)).astype(jnp.bfloat16)

        @pl.when(jnp.logical_not(more))
        def _():
            zsend[o] = total.astype(jnp.bfloat16)
        z_copy(o, step).start()

    for o, here, step in order:
        pl.when(here)(functools.partial(to_z, o, step))

    total = chip_pair_sum(0) + res_ref[...].astype(jnp.float32)

    @pl.when(z == 0)
    def _():
        z_arrived(0, 1).wait_recv()
        out_ref[...] = (total + zrecv[1, 0].astype(jnp.float32)).astype(jnp.bfloat16)

    @pl.when(z == NZ - 1)
    def _():
        z_arrived(0, 0).wait_recv()
        out_ref[...] = (total + zrecv[0, 0].astype(jnp.float32)).astype(jnp.bfloat16)

    @pl.when(jnp.logical_and(z > 0, z < NZ - 1))
    def _():
        z_arrived(0, 0).wait_recv()
        z_arrived(0, 1).wait_recv()
        out_ref[...] = (total + zrecv[0, 0].astype(jnp.float32)
                        + zrecv[1, 0].astype(jnp.float32)).astype(jnp.bfloat16)

    for o in range(NZ):
        y_copy(o).wait_send()
        for yy in range(2):
            c_copy(o, yy).wait_send()
    for o, here, step in order:
        pl.when(here)(lambda o=o, step=step: z_copy(o, step).wait_send())


def reduce_blocks(parts, residual):
    _, _, rows, lanes = parts.shape
    dma = pltpu.SemaphoreType.DMA
    vmem = pl.BlockSpec(memory_space=pltpu.VMEM)
    buf = lambda *lead: pltpu.VMEM(lead + (rows, lanes), jnp.bfloat16)
    return pl.pallas_call(
        reduce_kernel,
        out_shape=jax.ShapeDtypeStruct((rows, lanes), jnp.bfloat16),
        in_specs=[vmem, vmem], out_specs=vmem,
        scratch_shapes=[buf(NZ, 2), buf(NZ), buf(NZ), buf(NZ), buf(2, NZ),
                        dma((NZ, 2)), dma((NZ, 2)), dma((NZ,)), dma((NZ,)), dma((NZ,)), dma((2, NZ))],
        compiler_params=pltpu.CompilerParams(collective_id=1, has_side_effects=True,
                                             vmem_limit_bytes=24 * 2**20),
        name="reduce_blocks",
    )(parts, residual)


def rope_rotate(vectors, positions):
    head_dim = vectors.shape[-1]
    half_dim = head_dim // 2
    inv_freq = ROPE_BASE ** (-2.0 * jnp.arange(half_dim, dtype=jnp.float32) / head_dim)
    angles = positions.astype(jnp.float32)[:, None] * inv_freq[None, :]
    bcast_shape = (angles.shape[0],) + (1,) * (vectors.ndim - 2) + (half_dim,)
    cos_part = jnp.cos(angles).reshape(bcast_shape)
    sin_part = jnp.sin(angles).reshape(bcast_shape)
    vec_f32 = vectors.astype(jnp.float32)
    first_half = vec_f32[..., :half_dim]
    second_half = vec_f32[..., half_dim:]
    rotated = jnp.concatenate([first_half * cos_part - second_half * sin_part, second_half * cos_part + first_half * sin_part], axis=-1)
    return rotated.astype(jnp.bfloat16)


def attend_rows(query_rot, key_rot, value_new, k_cache, v_cache, lengths):
    positions = jnp.arange(k_cache.shape[1], dtype=jnp.int32)
    write_mask = (positions[None, :] == lengths[:, None])[:, :, None]
    k_updated = jnp.where(write_mask, key_rot[:, None, :], k_cache)
    v_updated = jnp.where(write_mask, value_new[:, None, :], v_cache)
    scores = jnp.einsum('rhd,rtd->rht', query_rot, k_updated, preferred_element_type=jnp.float32) * (query_rot.shape[-1] ** -0.5)
    valid_mask = (positions[None, :] <= lengths[:, None])[:, None, :]
    scores = jnp.where(valid_mask, scores, -1e30)
    attn_probs = jax.nn.softmax(scores, axis=-1).astype(jnp.bfloat16)
    attended = jnp.einsum('rht,rtd->rhd', attn_probs, v_updated, preferred_element_type=jnp.float32).astype(jnp.bfloat16)
    return attended, k_updated, v_updated


def cut(w, axis, start, size):
    return lax.dynamic_slice_in_dim(w, start, size, axis=axis)


def dot00(a, b):
    return lax.dot_general(a, b, (((0,), (0,)), ((), ())), preferred_element_type=jnp.float32)


def solution(mesh):
    row_axes = ('dp', 'tx', 'tyz')
    tx_size = mesh.shape['tx']

    def decode_layer(residual, ln_scale, w_query, w_key, w_value, w_gate, w_up, w_out, w_down, k_cache, v_cache, lengths):
        dp, z, ty = lax.axis_index('dp'), lax.axis_index('tx'), lax.axis_index('tyz')
        rows_all, cols = residual.shape
        rows = k_cache.shape[0]
        head_dim = w_key.shape[1]
        model_dim = cols * 16
        k_slice = w_gate.shape[0]
        mlp_half = w_gate.shape[1] // tx_size // 2
        kv_half = 2 * head_dim // 16 // 2
        w_kv = jnp.concatenate([w_key.T, w_value.T], axis=0)
        wq_t = w_query.T

        def qkv_block(target, h):
            return jnp.concatenate([
                cut(wq_t, 0, target * 2 * head_dim + h * head_dim, head_dim),
                cut(w_kv, 0, (target * 4 + ty) * 2 * kv_half + h * kv_half, kv_half)], axis=0)

        def mlp_block(target, h):
            at = (target * 2 + h) * mlp_half
            return jnp.concatenate([cut(w_gate, 1, at, mlp_half), cut(w_up, 1, at, mlp_half)], axis=1)

        def out_block(target, h):
            return jnp.concatenate([
                cut(w_down, 0, (target * 2 + h) * mlp_half, mlp_half),
                cut(w_out, 0, (target * 2 + h) * head_dim, head_dim)], axis=0)

        def exchange(block):
            mine, twin = [block(z, dp)], [block(z, 1 - dp)]
            for o in range(1, NZ):
                got = lax.ppermute(block(lax.rem(z + o, NZ), dp), 'tx', [(i, (i + o) % NZ) for i in range(NZ)])
                mine.append(got)
                twin.append(lax.ppermute(got, 'dp', [(0, 1), (1, 0)]))
            return mine, twin

        scale_rows = jnp.pad(ln_scale[None, :], ((0, EXTRA - 1), (0, rows_all - cols)))
        gathered = gather_blocks(jnp.concatenate([residual.T, scale_rows], axis=0))
        qkv_w = exchange(qkv_block)
        mlp_w = exchange(mlp_block)
        out_w = exchange(out_block)

        res_f32 = gathered[:, :, :cols, :].astype(jnp.float32)
        scale = gathered[:, :, cols, :cols].astype(jnp.float32)
        row_mean = jnp.sum(res_f32, axis=(0, 1, 2)) / model_dim
        row_var = jnp.sum(jnp.square(res_f32 - row_mean), axis=(0, 1, 2)) / model_dim
        normed = ((res_f32 - row_mean) * lax.rsqrt(row_var + LN_EPS) * scale[..., None]).astype(jnp.bfloat16)
        normed = normed.reshape(NZ, 4 * cols, rows_all)

        qkv = []
        for ws in qkv_w:
            acc = sum(jnp.dot(ws[o], normed[o], preferred_element_type=jnp.float32) for o in range(NZ))
            qkv.append(acc.astype(jnp.bfloat16))
        qkv = jnp.concatenate(qkv, axis=0)
        qkv = qkv.reshape(qkv.shape[0], 16, rows).transpose(1, 0, 2)
        qkv = lax.all_to_all(qkv, ('tx', 'tyz'), 0, 0, tiled=True)
        half = head_dim + kv_half
        qkv = qkv.reshape(16, 2, half, rows)
        query = qkv[:, :, :head_dim].reshape(32, head_dim, rows).transpose(2, 0, 1)
        kv = qkv[:, :, head_dim:]
        kv = jnp.where(dp == 0, kv, kv[:, ::-1]).reshape(2 * head_dim, rows).T
        query_rot = rope_rotate(query, lengths)
        key_rot = rope_rotate(kv[:, :head_dim], lengths)
        attended, k_updated, v_updated = attend_rows(query_rot, key_rot, kv[:, head_dim:], k_cache, v_cache, lengths)
        attn = attended.reshape(rows, 16, 2 * head_dim).transpose(1, 0, 2)
        attn = lax.all_to_all(attn, ('tx', 'tyz'), 0, 0, tiled=True).reshape(rows_all, 2, head_dim)

        parts = [0.0] * NZ
        for h, ws in enumerate(mlp_w):
            acc = sum(dot00(normed[o], ws[o]) for o in range(NZ)).astype(jnp.bfloat16)
            gate, up = acc[:, :mlp_half].astype(jnp.float32), acc[:, mlp_half:].astype(jnp.float32)
            act = (jax.nn.silu(gate) * up).astype(jnp.bfloat16)
            lhs = jnp.concatenate([act, attn[:, h]], axis=1)
            for o in range(NZ):
                parts[o] = parts[o] + lax.dot_general(
                    out_w[h][o], lhs, (((0,), (1,)), ((), ())), preferred_element_type=jnp.float32)
        parts = jnp.stack([p.astype(jnp.bfloat16) for p in parts]).reshape(NZ, 4, cols, rows_all)
        new_resid = reduce_blocks(parts, residual.T).T
        return new_resid, k_updated, v_updated

    full = P(row_axes)
    res_spec = P('dp', ('tx', 'tyz'))
    return jax.shard_map(
        decode_layer, mesh=mesh,
        in_specs=(res_spec, P(('tx', 'tyz')), P('tx', 'tyz'), P('tx'), P('tx'), P('tx', 'tyz'), P('tx', 'tyz'),
                  P('tyz', 'tx'), P('tyz', 'tx'), full, full, full),
        out_specs=(res_spec, full, full), check_vma=False)
```

time: 515 us -> 371 us (0.72)
  waiting for transfers between devices: 345 us -> 88.8 us
  Pallas kernels: 0 us -> 109 us
  blocking collectives: 47.1 us -> 0 us
  starting transfers between devices: 4.02 us -> 35.7 us
  between operations: 14 us -> 1.67 us
  other arithmetic: 30.8 us -> 43.1 us
  matrix products: 47.7 us -> 56.4 us
  local copies, waits for them, and re-layouts: 25.6 us -> 32.8 us
    unnamed x11 -> x0, waiting for transfers between devices: 167 us -> none
    pallas_call x0 -> x2, Pallas kernels: none -> 109 us  [the longest x1 70.8 us: gather_blocks(): pl.pallas_call(gather_kernel, out_shape=jax.ShapeDtypeStruct((NZ, 4, rows...]
    reduce_scatter x4 -> x0, waiting for transfers between devices: 94.4 us -> none  [the longest x1 31.3 us: decode_layer(): lax.psum_scatter(query_part, 'tx', scatter_dimension=0, tiled=True)]
    all_gather x3 -> x0, waiting for transfers between devices: 83.7 us -> none  [the longest x1 41.7 us: decode_layer(): act_full = lax.all_gather(mlp_act, 'tx', axis=1, tiled=True)]
    ppermute x0 -> x18, waiting for transfers between devices: none -> 75.5 us  [the longest x9 50.2 us: exchange(): lax.ppermute(block(lax.rem(z + o, NZ), dp), 'tx', [(i, (i + o) % NZ) for...]
    psum x1 -> x0, blocking collectives: 35.5 us -> none  [decode_layer(): row_stats = lax.psum(row_stats, ('tx', 'tyz'))]
    ppermute x0 -> x18, starting transfers between devices: none -> 26.2 us  [the longest x9 15.8 us: exchange(): lax.ppermute(block(lax.rem(z + o, NZ), dp), 'tx', [(i, (i + o) % NZ) for...]
    all_to_all x1 -> x2, waiting for transfers between devices: 0.01 us -> 13.4 us  [the longest x1 7.73 us: decode_layer(): lax.all_to_all(attn, ('tx', 'tyz'), 0, 0, tiled=True)]
  transfers between devices with their start and end apart: 10 -> 20, of which waited for: 9 -> 9; matrix products, arithmetic and copies ran while one was open for 15% -> 32% of each run, Pallas kernels for 0% -> 19%
where the time goes in v1:
time: 371 us; the launch traced here: 367 us
  Pallas kernels  109 us (29%)
  waiting for transfers between devices  88.8 us (24%)
  matrix products  56.4 us (15%)
  other arithmetic  43.1 us (12%)
  starting transfers between devices  35.7 us (10%)
  local copies, waits for them, and re-layouts  32.8 us (9%)
    pallas_call x1, Pallas kernels, gather_blocks(): pl.pallas_call(gather_kernel, out_shape=jax.ShapeDtypeStruct((NZ, 4, rows...  70.8 us
    ppermute x9, waiting for transfers between devices, exchange(): lax.ppermute(block(lax.rem(z + o, NZ), dp), 'tx', [(i, (i + o) % NZ) for...  50.2 us
    pallas_call x1, Pallas kernels, reduce_blocks(): pl.pallas_call(reduce_kernel, out_shape=jax.ShapeDtypeStruct((rows, lanes...  37.9 us
    ppermute x9, waiting for transfers between devices, exchange(): twin.append(lax.ppermute(got, 'dp', [(0, 1), (1, 0)]))  25.3 us
    dot_general x8, matrix products, dot00(): lax.dot_general(a, b, (((0,), (0,)), ((), ())), preferred_element_type=jn...  24.3 us
    ppermute x9, starting transfers between devices, exchange(): lax.ppermute(block(lax.rem(z + o, NZ), dp), 'tx', [(i, (i + o) % NZ) for...  15.8 us
    dot_general x8, matrix products, decode_layer(): lax.dot_general(out_w[h][o], lhs, (((0,), (1,)), ((), ())), preferred_ele...  14.2 us
    select_n x1, other arithmetic, attend_rows(): k_updated = jnp.where(write_mask, key_rot[:, None, :], k_cache)  12.9 us
  transfers between devices with their start and end apart: 20, of which 9 were waited for; matrix products, arithmetic and copies ran while one was open for 32% of the time, Pallas kernels for 19%

profile of v1, /device:TPU:0, one launch (start us, length us, event | category | flops | bytes accessed | tf_op | source)
XLA Modules:
  0.0 367.2 jit_solution(2487744821670613137)
XLA Ops:
  1.8 2.6 dynamic-slice_bitcast_fusion.4
  5.2 4.0 %collective-permute-start.4 = (bf16[85,640]{0,1:T(8,128)(2,1)}, bf16[85,640]{0,1:T(8,128)(2,1)}, u32[]{:S(2)}, u32[]{:S(2)}) collective-permute-start(bf16[85,640]{0,1:T(8,128)(2,1)} %pad_maximum_fusion.11), channel_id=1, source_target_pairs={{0,8},{4,12},{8,0},{12,4},{1,9},{5,13},{9,1},{13,5},{2,10},{6,14},... | collective-permute-start | bytes 326408 | tf_op jit(solution)/shard_map/ppermute | solution.py:312
  23.0 70.8 %gather_blocks.1 = bf16[4,4,176,1024]{3,2,1,0:T(8,128)(2,1)S(1)} custom-call(bf16[176,1024]{1,0:T(8,128)(2,1)S(1)} %fusion.46.x_ref), custom_call_target="tpu_custom_call" | custom-call | tf_op jit(solution)/shard_map/gather_blocks/pallas_call | solution.py:116
  98.0 3.9 %fusion.3 = f32[1024]{0:T(1024)S(1)} fusion(f32[1024]{0:T(1024)S(1)} %broadcast_multiply_fusion, bf16[4,4,176,1024]{3,2,1,0:T(8,128)(2,1)} %copy-done), kind=kLoop, calls=%fused_computation.5 | loop fusion | flops 10484736 | bytes 5251072 | tf_op jit(solution)/shard_map/reduce_sum | solution.py:326
  101.9 4.0 %fusion.5 = bf16[4,4,160,1024]{3,2,1,0:T(8,128)(2,1)S(1)} fusion(f32[4,4,160]{2,1,0:T(4,128)S(1)} %bitcast.113, f32[1024]{0:T(1024)S(1)} %add_rsqrt_fusion, f32[1024]{0:T(1024)S(1)} %broadcast_multiply_fusion, bf16[4,4,176,1024]{3,2,1,0:T(8,128)(2,1)} %copy-done), kind=kLoop, calls=%fused_computation.7 | loop fusion | flops 13107200 | bytes 10504192 | tf_op jit(solution)/shard_map/convert_element_type | solution.py:327
  109.6 2.9 constant_dynamic-slice_fusion.6
  117.0 2.8 fusion.30
  119.8 2.8 fusion.26
  141.8 4.2 %all-to-all-start = ((bf16[16,170,64]{1,2,0:T(8,128)(2,1)}), bf16[16,170,64]{1,2,0:T(8,128)(2,1)}, u32[]{:S(2)}, u32[]{:S(2)}) async-start(bf16[16,170,64]{1,2,0:T(8,128)(2,1)} %bitcast.13), calls=%async_computation | async-start | bytes 1048576 | tf_op jit(solution)/shard_map/all_to_all | solution.py:336
  149.3 12.5 %collective-permute-done.1 = bf16[640,640]{1,0:T(8,128)(2,1)} collective-permute-done((bf16[640,640]{1,0:T(8,128)(2,1)}, bf16[640,640]{1,0:T(8,128)(2,1)}, u32[]{:S(2)}, u32[]{:S(2)}) %collective-permute-start.1) | collective-permute-done | bytes 819232 | tf_op jit(solution)/shard_map/ppermute | solution.py:312
  163.2 3.8 %fusion.76 = f32[1024,640]{0,1:T(8,128)} fusion(bf16[640,1024]{1,0:T(8,128)(2,1)S(1)} %bitcast.86, bf16[640,640]{1,0:T(8,128)(2,1)} %collective-permute-done.1), kind=kOutput, calls=%fused_computation.164 | convolution fusion | flops 838860800 | bytes 4751360 | tf_op jit(solution)/shard_map/dot_general | solution.py:276
  167.0 37.6 %collective-permute-done.2 = bf16[640,640]{1,0:T(8,128)(2,1)} collective-permute-done((bf16[640,640]{1,0:T(8,128)(2,1)}, bf16[640,640]{1,0:T(8,128)(2,1)}, u32[]{:S(2)}, u32[]{:S(2)}) %collective-permute-start.2) | collective-permute-done | bytes 819232 | tf_op jit(solution)/shard_map/ppermute | solution.py:312
  206.7 3.9 %fusion.75 = f32[1024,640]{0,1:T(8,128)} fusion(bf16[640,1024]{1,0:T(8,128)(2,1)S(1)} %bitcast.90, bf16[640,640]{1,0:T(8,128)(2,1)} %collective-permute-done), kind=kOutput, calls=%fused_computation.163 | convolution fusion | flops 838860800 | bytes 4751360 | tf_op jit(solution)/shard_map/dot_general | solution.py:276
  210.6 5.6 %all-to-all-done = bf16[16,170,64]{1,2,0:T(8,128)(2,1)} async-done(((bf16[16,170,64]{1,2,0:T(8,128)(2,1)}), bf16[16,170,64]{1,2,0:T(8,128)(2,1)}, u32[]{:S(2)}, u32[]{:S(2)}) %all-to-all-start) | async-done | bytes 348192 | tf_op jit(solution)/shard_map/all_to_all | solution.py:336
  223.6 12.9 %broadcast_select_fusion.1 = (bf16[64,1024,80]{1,2,0:T(8,128)(2,1)S(1)}, bf16[64,1024,80]{1,2,0:T(8,128)(2,1)}) fusion(bf16[64,1024,80]{1,2,0:T(8,128)(2,1)} %param.21, pred[64,1024]{1,0:T(8,128)(4,1)S(1)} %copy-done.20, bf16[64,80]{1,0:T(8,128)(2,1)S(1)} %copy.46, bf16[64,1024,80]{1,2,0:T(8,128)(2,1)} %param.22, bf16[64,80]{1,0:T(8,128)(2,1)S(1)} %copy.47), kind=kLoop, calls=%fused_computation.9 | loop fusion | flops 10485760 | bytes 42029056 | tf_op jit(solution)/shard_map/jit(_where)/select_n | solution.py:261
  240.6 5.2 %fusion.74 = (f32[64,32]{1,0:T(8,128)S(1)}, f32[64,32,1024]{2,1,0:T(8,128)}) fusion(f32[64,32,1024]{2,1,0:T(8,128)S(1)} %fusion.35, pred[64,1024]{1,0:T(8,128)(4,1)S(1)} %copy-done.22), kind=kOutput, calls=%fused_computation.162 | output fusion | flops 12583935 | bytes 16850944 | tf_op jit(solution)/shard_map/sub | solution.py:266
  245.7 10.2 %fusion.21 = bf16[64,32,80]{2,1,0:T(8,128)(2,1)} fusion(bf16[64,1024,80]{1,2,0:T(8,128)(2,1)} %get-tuple-element.65, f32[64,32,1024]{2,1,0:T(8,128)} %get-tuple-element.54, f32[64,32]{1,0:T(8,128)S(1)} %get-tuple-element.53), kind=kOutput, calls=%fused_computation.39 | convolution fusion | flops 339902464 | bytes 19210240 | tf_op jit(solution)/shard_map/rht,rtd->rhd/dot_general | solution.py:267
  258.3 5.2 %all-to-all-start.1 = ((bf16[16,64,160]{2,1,0:T(8,128)(2,1)}), bf16[16,64,160]{2,1,0:T(8,128)(2,1)}, u32[]{:S(2)}, u32[]{:S(2)}) async-start(bf16[16,64,160]{2,1,0:T(8,128)(2,1)} %bitcast.74), calls=%async_computation.1 | async-start | bytes 1048576 | tf_op jit(solution)/shard_map/all_to_all | solution.py:346
  263.5 4.9 %add_convert_fusion.5 = bf16[1024,640]{0,1:T(8,128)(2,1)S(1)} fusion(f32[1024,640]{0,1:T(8,128)} %fusion.76, f32[1024,640]{0,1:T(8,128)} %fusion.26, f32[1024,640]{0,1:T(8,128)} %fusion.75, bf16[640,1024]{1,0:T(8,128)(2,1)S(1)} %bitcast.82, bf16[640,640]{1,0:T(8,128)(2,1)} %collective-permute-done.2), kind=kOutput, calls=%fused_computation.24 | convolution fusion | flops 841482240 | bytes 11304960 | tf_op jit(solution)/shard_map/dot_general | solution.py:276
  269.7 7.7 %all-to-all-done.1 = bf16[16,64,160]{2,1,0:T(8,128)(2,1)} async-done(((bf16[16,64,160]{2,1,0:T(8,128)(2,1)}), bf16[16,64,160]{2,1,0:T(8,128)(2,1)}, u32[]{:S(2)}, u32[]{:S(2)}) %all-to-all-start.1) | async-done | bytes 327712 | tf_op jit(solution)/shard_map/all_to_all | solution.py:346
  281.7 3.6 fusion.70
  296.1 13.8 %collective-permute-done.9 = bf16[640,640]{1,0:T(8,128)(2,1)S(1)} collective-permute-done((bf16[640,640]{1,0:T(8,128)(2,1)}, bf16[640,640]{1,0:T(8,128)(2,1)S(1)}, u32[]{:S(2)}, u32[]{:S(2)}) %collective-permute-start.9) | collective-permute-done | bytes 819232 | tf_op jit(solution)/shard_map/ppermute | solution.py:314
  314.6 6.1 %collective-permute-done.13 = bf16[400,640]{1,0:T(8,128)(2,1)S(1)} collective-permute-done((bf16[400,640]{1,0:T(8,128)(2,1)}, bf16[400,640]{1,0:T(8,128)(2,1)S(1)}, u32[]{:S(2)}, u32[]{:S(2)}) %collective-permute-start.13) | collective-permute-done | bytes 512032 | tf_op jit(solution)/shard_map/ppermute | solution.py:314
  328.3 37.9 %reduce_blocks.1 = bf16[160,1024]{1,0:T(8,128)(2,1)S(1)} custom-call(bf16[4,4,160,1024]{3,2,1,0:T(8,128)(2,1)S(1)} %pad_maximum_fusion.p_ref, bf16[160,1024]{1,0:T(8,128)(2,1)S(1)} %bitcast.78), custom_call_target="tpu_custom_call" | custom-call | tf_op jit(solution)/shard_map/reduce_blocks/pallas_call | solution.py:231
  (155 shorter events, 96.2 us)
Async XLA Ops:
  1.8 13.2 %copy-start.19 = (bf16[640,640]{1,0:T(8,128)(2,1)S(1)}, bf16[640,640]{1,0:T(8,128)(2,1)}, u32[]{:S(2)}) copy-start(bf16[640,640]{1,0:T(8,128)(2,1)} %param.19) | copy-start | bytes 2457604
  5.2 119.1 %collective-permute-start.4 = (bf16[85,640]{0,1:T(8,128)(2,1)}, bf16[85,640]{0,1:T(8,128)(2,1)}, u32[]{:S(2)}, u32[]{:S(2)}) collective-permute-start(bf16[85,640]{0,1:T(8,128)(2,1)} %pad_maximum_fusion.11), channel_id=1, source_target_pairs={{0,8},{4,12},{8,0},{12,4},{1,9},{5,13},{9,1},{13,5},{2,10},{6,14},... | collective-permute-start | bytes 326408 | tf_op jit(solution)/shard_map/ppermute | solution.py:312
  10.2 112.4 %collective-permute-start.3 = (bf16[85,640]{0,1:T(8,128)(2,1)}, bf16[85,640]{0,1:T(8,128)(2,1)}, u32[]{:S(2)}, u32[]{:S(2)}) collective-permute-start(bf16[85,640]{0,1:T(8,128)(2,1)} %pad_maximum_fusion.10), channel_id=1, source_target_pairs={{0,4},{4,8},{8,12},{12,0},{1,5},{5,9},{9,13},{13,1},{2,6},{6,10},{... | collective-permute-start | bytes 326408 | tf_op jit(solution)/shard_map/ppermute | solution.py:312
  12.7 113.2 %collective-permute-start.5 = (bf16[85,640]{0,1:T(8,128)(2,1)}, bf16[85,640]{0,1:T(8,128)(2,1)}, u32[]{:S(2)}, u32[]{:S(2)}) collective-permute-start(bf16[85,640]{0,1:T(8,128)(2,1)} %pad_maximum_fusion.12), channel_id=1, source_target_pairs={{0,12},{4,0},{8,4},{12,8},{1,13},{5,1},{9,5},{13,9},{2,14},{6,2},{... | collective-permute-start | bytes 326408 | tf_op jit(solution)/shard_map/ppermute | solution.py:312
  19.2 126.8 %collective-permute-start.14 = (bf16[400,640]{1,0:T(8,128)(2,1)}, bf16[400,640]{1,0:T(8,128)(2,1)}, u32[]{:S(2)}, u32[]{:S(2)}) collective-permute-start(bf16[400,640]{1,0:T(8,128)(2,1)} %pad_maximum_fusion.7), channel_id=1, source_target_pairs={{0,8},{4,12},{8,0},{12,4},{1,9},{5,13},{9,1},{13,5},{2,10},{6,14},... | collective-permute-start | bytes 1536008 | tf_op jit(solution)/shard_map/ppermute | solution.py:312
  20.1 127.8 %collective-permute-start.16 = (bf16[400,640]{1,0:T(8,128)(2,1)}, bf16[400,640]{1,0:T(8,128)(2,1)}, u32[]{:S(2)}, u32[]{:S(2)}) collective-permute-start(bf16[400,640]{1,0:T(8,128)(2,1)} %pad_maximum_fusion.8), channel_id=1, source_target_pairs={{0,12},{4,0},{8,4},{12,8},{1,13},{5,1},{9,5},{13,9},{2,14},{6,2},{... | collective-permute-start | bytes 1536008 | tf_op jit(solution)/shard_map/ppermute | solution.py:312
  106.6 26.4 %copy-start.3 = (bf16[1,4,160,1024]{3,2,1,0:T(8,128)(2,1)}, bf16[1,4,160,1024]{3,2,1,0:T(8,128)(2,1)S(1)}, u32[]{:S(2)}) copy-start(bf16[1,4,160,1024]{3,2,1,0:T(8,128)(2,1)S(1)} %get-tuple-element.5) | copy-start | bytes 3932164
  122.6 39.2 %collective-permute-start.1 = (bf16[640,640]{1,0:T(8,128)(2,1)}, bf16[640,640]{1,0:T(8,128)(2,1)}, u32[]{:S(2)}, u32[]{:S(2)}) collective-permute-start(bf16[640,640]{1,0:T(8,128)(2,1)} %pad_maximum_fusion.2), channel_id=1, source_target_pairs={{0,8},{4,12},{8,0},{12,4},{1,9},{5,13},{9,1},{13,5},{2,10},{6,14},... | collective-permute-start | bytes 2457608 | tf_op jit(solution)/shard_map/ppermute | solution.py:312
  124.5 7.1 %collective-permute-start.6 = (bf16[85,640]{0,1:T(8,128)(2,1)}, bf16[85,640]{0,1:T(8,128)(2,1)S(1)}, u32[]{:S(2)}, u32[]{:S(2)}) collective-permute-start(bf16[85,640]{0,1:T(8,128)(2,1)} %collective-permute-done.3), channel_id=1, source_target_pairs={{0,16},{16,0},{1,17},{17,1},{2,18},{18,2},{3,19},{19,3},{4,20},{20... | collective-permute-start | bytes 326408 | tf_op jit(solution)/shard_map/ppermute | solution.py:314
  125.9 9.2 %collective-permute-start.7 = (bf16[85,640]{0,1:T(8,128)(2,1)}, bf16[85,640]{0,1:T(8,128)(2,1)S(1)}, u32[]{:S(2)}, u32[]{:S(2)}) collective-permute-start(bf16[85,640]{0,1:T(8,128)(2,1)} %collective-permute-done.4), channel_id=1, source_target_pairs={{0,16},{16,0},{1,17},{17,1},{2,18},{18,2},{3,19},{19,3},{4,20},{20... | collective-permute-start | bytes 326408 | tf_op jit(solution)/shard_map/ppermute | solution.py:314
  131.7 6.1 %collective-permute-start.8 = (bf16[85,640]{0,1:T(8,128)(2,1)}, bf16[85,640]{0,1:T(8,128)(2,1)S(1)}, u32[]{:S(2)}, u32[]{:S(2)}) collective-permute-start(bf16[85,640]{0,1:T(8,128)(2,1)} %collective-permute-done.5), channel_id=1, source_target_pairs={{0,16},{16,0},{1,17},{17,1},{2,18},{18,2},{3,19},{19,3},{4,20},{20... | collective-permute-start | bytes 326408 | tf_op jit(solution)/shard_map/ppermute | solution.py:314
  135.2 69.5 %collective-permute-start.2 = (bf16[640,640]{1,0:T(8,128)(2,1)}, bf16[640,640]{1,0:T(8,128)(2,1)}, u32[]{:S(2)}, u32[]{:S(2)}) collective-permute-start(bf16[640,640]{1,0:T(8,128)(2,1)} %pad_maximum_fusion.3), channel_id=1, source_target_pairs={{0,12},{4,0},{8,4},{12,8},{1,13},{5,1},{9,5},{13,9},{2,14},{6,2},{... | collective-permute-start | bytes 2457608 | tf_op jit(solution)/shard_map/ppermute | solution.py:312
  137.8 68.2 %collective-permute-start = (bf16[640,640]{1,0:T(8,128)(2,1)}, bf16[640,640]{1,0:T(8,128)(2,1)}, u32[]{:S(2)}, u32[]{:S(2)}) collective-permute-start(bf16[640,640]{1,0:T(8,128)(2,1)} %pad_maximum_fusion.1), channel_id=1, source_target_pairs={{0,4},{4,8},{8,12},{12,0},{1,5},{5,9},{9,13},{13,1},{2,6},{6,10},{... | collective-permute-start | bytes 2457608 | tf_op jit(solution)/shard_map/ppermute | solution.py:312
  141.8 74.4 %all-to-all-start = ((bf16[16,170,64]{1,2,0:T(8,128)(2,1)}), bf16[16,170,64]{1,2,0:T(8,128)(2,1)}, u32[]{:S(2)}, u32[]{:S(2)}) async-start(bf16[16,170,64]{1,2,0:T(8,128)(2,1)} %bitcast.13), calls=%async_computation | async-start | bytes 1048576 | tf_op jit(solution)/shard_map/all_to_all | solution.py:336
  146.0 60.6 %copy-start.4 = (bf16[1,4,160,1024]{3,2,1,0:T(8,128)(2,1)S(1)}, bf16[1,4,160,1024]{3,2,1,0:T(8,128)(2,1)}, u32[]{:S(2)}) copy-start(bf16[1,4,160,1024]{3,2,1,0:T(8,128)(2,1)} %copy-done.3) | copy-start | bytes 3932164
  146.1 142.7 %collective-permute-start.12 = (bf16[400,640]{1,0:T(8,128)(2,1)}, bf16[400,640]{1,0:T(8,128)(2,1)}, u32[]{:S(2)}, u32[]{:S(2)}) collective-permute-start(bf16[400,640]{1,0:T(8,128)(2,1)} %pad_maximum_fusion.6), channel_id=1, source_target_pairs={{0,4},{4,8},{8,12},{12,0},{1,5},{5,9},{9,13},{13,1},{2,6},{6,10},{... | collective-permute-start | bytes 1536008 | tf_op jit(solution)/shard_map/ppermute | solution.py:312
  147.9 174.8 %collective-permute-start.15 = (bf16[400,640]{1,0:T(8,128)(2,1)}, bf16[400,640]{1,0:T(8,128)(2,1)}, u32[]{:S(2)}, u32[]{:S(2)}) collective-permute-start(bf16[400,640]{1,0:T(8,128)(2,1)} %collective-permute-done.14), channel_id=1, source_target_pairs={{0,16},{16,0},{1,17},{17,1},{2,18},{18,2},{3,19},{19,3},{4,20},{20... | collective-permute-start | bytes 1536008 | tf_op jit(solution)/shard_map/ppermute | solution.py:314
  161.8 163.7 %collective-permute-start.17 = (bf16[400,640]{1,0:T(8,128)(2,1)}, bf16[400,640]{1,0:T(8,128)(2,1)}, u32[]{:S(2)}, u32[]{:S(2)}) collective-permute-start(bf16[400,640]{1,0:T(8,128)(2,1)} %collective-permute-done.16), channel_id=1, source_target_pairs={{0,16},{16,0},{1,17},{17,1},{2,18},{18,2},{3,19},{19,3},{4,20},{20... | collective-permute-start | bytes 1536008 | tf_op jit(solution)/shard_map/ppermute | solution.py:314
  204.6 88.4 %collective-permute-start.10 = (bf16[640,640]{1,0:T(8,128)(2,1)}, bf16[640,640]{1,0:T(8,128)(2,1)}, u32[]{:S(2)}, u32[]{:S(2)}) collective-permute-start(bf16[640,640]{1,0:T(8,128)(2,1)} %collective-permute-done.1), channel_id=1, source_target_pairs={{0,16},{16,0},{1,17},{17,1},{2,18},{18,2},{3,19},{19,3},{4,20},{20... | collective-permute-start | bytes 2457608 | tf_op jit(solution)/shard_map/ppermute | solution.py:314
  206.0 105.2 %collective-permute-start.11 = (bf16[640,640]{1,0:T(8,128)(2,1)}, bf16[640,640]{1,0:T(8,128)(2,1)}, u32[]{:S(2)}, u32[]{:S(2)}) collective-permute-start(bf16[640,640]{1,0:T(8,128)(2,1)} %collective-permute-done.2), channel_id=1, source_target_pairs={{0,16},{16,0},{1,17},{17,1},{2,18},{18,2},{3,19},{19,3},{4,20},{20... | collective-permute-start | bytes 2457608 | tf_op jit(solution)/shard_map/ppermute | solution.py:314
  258.3 19.2 %all-to-all-start.1 = ((bf16[16,64,160]{2,1,0:T(8,128)(2,1)}), bf16[16,64,160]{2,1,0:T(8,128)(2,1)}, u32[]{:S(2)}, u32[]{:S(2)}) async-start(bf16[16,64,160]{2,1,0:T(8,128)(2,1)} %bitcast.74), calls=%async_computation.1 | async-start | bytes 1048576 | tf_op jit(solution)/shard_map/all_to_all | solution.py:346
  288.8 21.2 %collective-permute-start.9 = (bf16[640,640]{1,0:T(8,128)(2,1)}, bf16[640,640]{1,0:T(8,128)(2,1)S(1)}, u32[]{:S(2)}, u32[]{:S(2)}) collective-permute-start(bf16[640,640]{1,0:T(8,128)(2,1)} %collective-permute-done), channel_id=1, source_target_pairs={{0,16},{16,0},{1,17},{17,1},{2,18},{18,2},{3,19},{19,3},{4,20},{20... | collective-permute-start | bytes 2457608 | tf_op jit(solution)/shard_map/ppermute | solution.py:314
  293.0 17.0 %copy-start.5 = (bf16[1,4,160,1024]{3,2,1,0:T(8,128)(2,1)S(1)}, bf16[1,4,160,1024]{3,2,1,0:T(8,128)(2,1)}, u32[]{:S(2)}) copy-start(bf16[1,4,160,1024]{3,2,1,0:T(8,128)(2,1)} %copy-done.3) | copy-start | bytes 3932164
  293.0 27.8 %collective-permute-start.13 = (bf16[400,640]{1,0:T(8,128)(2,1)}, bf16[400,640]{1,0:T(8,128)(2,1)S(1)}, u32[]{:S(2)}, u32[]{:S(2)}) collective-permute-start(bf16[400,640]{1,0:T(8,128)(2,1)} %collective-permute-done.12), channel_id=1, source_target_pairs={{0,16},{16,0},{1,17},{17,1},{2,18},{18,2},{3,19},{19,3},{4,20},{20... | collective-permute-start | bytes 1536008 | tf_op jit(solution)/shard_map/ppermute | solution.py:314
  (21 other events, 56.4 us)

commit v2 on v0

v2 whole, which is shorter than its diff:
```python
import jax
import jax.numpy as jnp
from jax import lax
from jax.experimental import pallas as pl
from jax.experimental.pallas import tpu as pltpu
from jax.sharding import PartitionSpec as P


LN_EPS = 1e-5
ROPE_BASE = 10000.0
NZ = 4
LANES = 128


def position():
    dp = lax.axis_index("dp")
    z = lax.axis_index("tx")
    ty = lax.axis_index("tyz")
    return dp, z, ty


def others(z, ty):
    for dz in (2, 1, 3, 0):
        for dt in range(4):
            if dz or dt:
                yield dz * 4 + dt - 1, lax.rem(z + dz, NZ), lax.rem(ty + dt, 4)


def source(z, ty, dz, dt):
    return lax.rem(z + NZ - dz, NZ) * 4 + lax.rem(ty + 4 - dt, 4)


def group_barrier(dp, z, ty):
    sem = pltpu.get_barrier_semaphore()
    for _, zt, tt in others(z, ty):
        pl.semaphore_signal(sem, inc=1, device_id=(dp, zt, tt), device_id_type=pl.DeviceIdType.MESH)
    pl.semaphore_signal(sem, inc=1, device_id=(1 - dp, z, ty), device_id_type=pl.DeviceIdType.MESH)
    pl.semaphore_wait(sem, 16)


def remote(src, dst, send_sem, recv_sem, device):
    return pltpu.make_async_remote_copy(src, dst, send_sem, recv_sem, device_id=device,
                                        device_id_type=pl.DeviceIdType.MESH)


def half_rows(dp, size, start=0):
    return pl.ds(pl.multiple_of(dp * size + start, 16), size)


def swap_halves(a, b, low):
    return jnp.where(low, a, pltpu.roll(b, 64, axis=1)), jnp.where(low, pltpu.roll(a, 64, axis=1), b)


def dot00(a, b):
    return lax.dot_general(a, b, (((0,), (0,)), ((), ())), preferred_element_type=jnp.float32)


GATE_EARLY = (1, 3)
LATE = ((0, 2), (1, 2), (1, 1), (1, 3))
TWINNED = 2


def first_kernel(x_ref, wqkv_ref, wg_ref, hn_ref, qkv_ref, gate_ref,
                 gat, wq, q32, packets, lsem, zs, zr, ys, yr, cs, cr,
                 qs, qr, qxs, qxr, gs, gr, gxs, gxr, as_, ar):
    dp, z, ty = position()
    y, c = ty // 2, lax.rem(ty, 2)
    peer_y, peer_c, twin = (1 - y) * 2 + c, y * 2 + 1 - c, (1 - dp, z, ty)
    f32, bf16 = jnp.float32, jnp.bfloat16
    cols, rows = x_ref.shape[0], hn_ref.shape[2]
    width = 4 * cols
    local_x = pltpu.make_async_copy(x_ref, gat.at[0, ty], lsem.at[0])
    local_w = pltpu.make_async_copy(wqkv_ref.at[z], wq.at[:, pl.ds(0, width)], lsem.at[1])
    local_x.start()
    local_w.start()
    group_barrier(dp, z, ty)

    def z_copy(o, step):
        slot = lax.rem(o + step + NZ, NZ)
        return remote(gat.at[o, ty], gat.at[slot, ty], zs.at[o, (step + 1) // 2], zr.at[slot], (dp, z + step, ty))

    def z_arrived(o):
        return remote(gat.at[o, ty], gat.at[o, ty], zs.at[o, 0], zr.at[o], (dp, z, peer_y))

    def y_copy(o, t=ty):
        return remote(gat.at[o, t], gat.at[o, t], ys.at[o], yr.at[o], (dp, z, peer_y))

    def c_copy(o, yy, core=c):
        t = yy * 2 + core
        return remote(gat.at[o, t], gat.at[o, t], cs.at[o, yy], cr.at[o, yy], (dp, z, peer_c))

    head = 80

    def q_copy(o):
        target = lax.rem(z + o, NZ)
        mine = half_rows(dp, head)
        to = (dp, target, ty)
        at = pl.ds(o * width, width)
        return (remote(wqkv_ref.at[target, mine], wq.at[mine, at], qs.at[o, 0], qr.at[o, 0], to),
                remote(wqkv_ref.at[target, pl.ds(2 * head, 16)], wq.at[pl.ds(2 * head, 16), at],
                       qs.at[o, 1], qr.at[o, 1], to))

    def q_pass(o, h):
        part = wq.at[half_rows(h, head), pl.ds(o * width, width)]
        return remote(part, part, qxs.at[o], qxr.at[o], twin)

    half_k = width // 2

    def g_copy(n, o):
        target = lax.rem(z + o, NZ)
        mine = half_rows(dp, half_k)
        return remote(wg_ref.at[mine, pl.ds(pl.multiple_of(target * width, LANES), width)],
                      gate_ref.at[n, mine], gs.at[n], gr.at[n], (dp, target, ty))

    def g_pass(n, h):
        part = gate_ref.at[n, half_rows(h, half_k)]
        return remote(part, part, gxs.at[n], gxr.at[n], twin)

    local_x.wait()
    pl.when(z < NZ - 1)(lambda: z_copy(0, 1).start())
    pl.when(z > 0)(lambda: z_copy(0, -1).start())
    y_copy(0).start()
    c_copy(0, y).start()
    for d in range(1, NZ):
        for o, here, onward, step in (
                (d, z >= d, z < NZ - 1, 1), (NZ - d, z + d < NZ, z > 0, -1)):
            @pl.when(here)
            def _(o=o, onward=onward, step=step):
                z_arrived(o).wait_recv()
                pl.when(onward)(lambda: z_copy(o, step).start())
                y_copy(o).start()
                c_copy(o, y).start()
    for o in (2, 1, 3):
        for copy in q_copy(o):
            copy.start()
    for n, o in enumerate(GATE_EARLY):
        g_copy(n, o).start()
    for d in range(NZ):
        for o, here in ((d, z >= d), (NZ - d, z + d < NZ)):
            if o < NZ:
                @pl.when(here if d else z >= 0)
                def _(o=o):
                    y_copy(o, peer_y).wait_recv()
                    c_copy(o, 1 - y).start()
    for o in (2, 1, 3):
        q_copy(o)[0].wait_recv()
        q_pass(o, dp).start()
    for o in range(NZ):
        for yy in range(2):
            c_copy(o, yy, 1 - c).wait_recv()
    for o in range(NZ):
        y_copy(o).wait_send()
        for yy in range(2):
            c_copy(o, yy).wait_send()

    def fold(v):
        return v.reshape(v.shape[0] // 8, 8, v.shape[1]).sum(axis=0)

    def block(i):
        return gat[i // 4, lax.rem(i, 4), :, pl.ds(0, rows)].astype(f32)

    total = lax.fori_loop(0, 16, lambda i, s: s + fold(block(i)), jnp.zeros((8, rows), f32))
    mean = jnp.sum(total, axis=0, keepdims=True) / (16 * cols)
    total = lax.fori_loop(0, 16, lambda i, s: s + fold(jnp.square(block(i) - mean)), jnp.zeros((8, rows), f32))
    rstd = lax.rsqrt(jnp.sum(total, axis=0, keepdims=True) / (16 * cols) + LN_EPS)

    def normalize(i, carry):
        o, t = i // 4, lax.rem(i, 4)
        scale = gat[o, t, :, pl.ds(rows, LANES)].astype(f32)
        for k in range(rows // LANES):
            at = slice(k * LANES, (k + 1) * LANES)
            v = gat[o, t, :, at].astype(f32)
            hn_ref[o, pl.ds(pl.multiple_of(t * cols, 16), cols), at] = (
                (v - mean[:, at]) * rstd[:, at] * scale).astype(bf16)
        return carry

    lax.fori_loop(0, 16, normalize, 0)

    local_w.wait()
    for o in (2, 1, 3):
        q_copy(o)[1].wait_recv()
        q_pass(o, 1 - dp).wait_recv()
    acc = jnp.dot(wq[:, 0:width], hn_ref[0], preferred_element_type=f32)
    for o in range(1, NZ):
        acc += jnp.dot(wq[:, o * width:(o + 1) * width], hn_ref[o], preferred_element_type=f32)
    q32[...] = acc.astype(bf16).astype(f32)
    low = lax.broadcasted_iota(jnp.int32, (head, LANES), 1) < 64
    for b in range(8):
        at = slice(b * LANES, (b + 1) * LANES)
        even, odd = swap_halves(q32[0:head, at], q32[head:2 * head, at], low)
        kv = q32[2 * head:2 * head + 16, at]
        packets[2 * b] = jnp.concatenate([even, kv], axis=0).astype(bf16)
        packets[2 * b + 1] = jnp.concatenate([odd, kv], axis=0).astype(bf16)
    me = z * 4 + ty

    def a_copy(n, zt, tt):
        return remote(packets.at[zt * 4 + tt], qkv_ref.at[me], as_.at[n], ar.at[n], (dp, zt, tt))

    for n, zt, tt in others(z, ty):
        a_copy(n, zt, tt).start()
    qkv_ref[me] = packets[me]
    for n, o in enumerate(GATE_EARLY):
        g_copy(n, o).wait_recv()
        g_pass(n, dp).start()
    for n, zt, tt in others(z, ty):
        dz, dt = (n + 1) // 4, (n + 1) % 4
        s = source(z, ty, dz, dt)
        remote(packets.at[s], qkv_ref.at[s], as_.at[n], ar.at[n], (dp, zt, tt)).wait_recv()
    for n, o in enumerate(GATE_EARLY):
        g_pass(n, 1 - dp).wait_recv()
        g_pass(n, dp).wait_send()
        g_copy(n, o).wait_send()
    for n, zt, tt in others(z, ty):
        a_copy(n, zt, tt).wait_send()
    for o in range(1, NZ):
        for copy in q_copy(o):
            copy.wait_send()
        q_pass(o, dp).wait_send()
    pl.when(z < NZ - 1)(lambda: z_copy(0, 1).wait_send())
    pl.when(z > 0)(lambda: z_copy(0, -1).wait_send())
    for d in range(1, NZ):
        pl.when(jnp.logical_and(z >= d, z < NZ - 1))(lambda d=d: z_copy(d, 1).wait_send())
        pl.when(jnp.logical_and(z + d < NZ, z > 0))(lambda d=d: z_copy(NZ - d, -1).wait_send())


def first_stage(x_ext, wqkv, w_gate, rows):
    cols = x_ext.shape[0]
    width = 4 * cols
    dma, bf16 = pltpu.SemaphoreType.DMA, jnp.bfloat16
    early = len(GATE_EARLY)
    anywhere, vmem = pl.BlockSpec(memory_space=pl.ANY), pl.BlockSpec(memory_space=pltpu.VMEM)
    return pl.pallas_call(
        first_kernel,
        out_shape=(jax.ShapeDtypeStruct((NZ, width, rows), bf16),
                   jax.ShapeDtypeStruct((16, 96, LANES), bf16),
                   jax.ShapeDtypeStruct((early, width, width), bf16)),
        in_specs=[anywhere] * 3,
        out_specs=(vmem, vmem, anywhere),
        scratch_shapes=[
            pltpu.VMEM((NZ, 4) + x_ext.shape, bf16), pltpu.VMEM((176, NZ * width), bf16),
            pltpu.VMEM((176, rows), jnp.float32), pltpu.VMEM((16, 96, LANES), bf16),
            dma((2,)), dma((NZ, 2)), dma((NZ,)), dma((NZ,)), dma((NZ,)), dma((NZ, 2)), dma((NZ, 2)),
            dma((NZ, 2)), dma((NZ, 2)), dma((NZ,)), dma((NZ,)),
            dma((early,)), dma((early,)), dma((early,)), dma((early,)), dma((15,)), dma((15,))],
        compiler_params=pltpu.CompilerParams(collective_id=0, has_side_effects=True,
                                             vmem_limit_bytes=32 * 2**20),
        name="first_stage",
    )(x_ext, wqkv, w_gate)


def last_kernel(*refs):
    mine_refs, refs = refs[:len(LATE)], refs[len(LATE):]
    twin_refs, refs = refs[:TWINNED], refs[TWINNED:]
    (hn_ref, op_ref, gate_ref, wg_ref, wu_ref, wd_ref, wo_ref, res_ref, out_ref,
                wgu, wdo, wt, lhs, acc, orecv, parts, cbuf, ysend, yrecv, zsend, zrecv,
                lsem, os_, or_, ws, wr, xs, xr, lxs, lxr, cs, cr, ys, yr, zs, zr) = refs
    dp, z, ty = position()
    y, c = ty // 2, lax.rem(ty, 2)
    peer_y, peer_c, twin = (1 - y) * 2 + c, y * 2 + 1 - c, (1 - dp, z, ty)
    f32, bf16 = jnp.float32, jnp.bfloat16
    width = hn_ref.shape[1]
    half_k, head = width // 2, 80
    inner = jnp.logical_and(z > 0, z < NZ - 1)
    early = {o: n for n, o in enumerate(GATE_EARLY)}

    def target_cols(target):
        return pl.ds(pl.multiple_of(target * width, LANES), width)

    local = [pltpu.make_async_copy(wg_ref.at[:, target_cols(z)], wgu.at[0, 0], lsem.at[0]),
             pltpu.make_async_copy(wu_ref.at[:, target_cols(z)], wgu.at[1, 0], lsem.at[1]),
             pltpu.make_async_copy(wd_ref.at[pl.ds(pl.multiple_of(z * width, 16), width)],
                                   wdo.at[0, pl.ds(0, width)], lsem.at[2]),
             pltpu.make_async_copy(wo_ref.at[pl.ds(pl.multiple_of(z * 2 * head, 16), 2 * head)],
                                   wdo.at[0, pl.ds(width, 2 * head)], lsem.at[3])]
    local += [pltpu.make_async_copy(gate_ref.at[n], wgu.at[0, o], lsem.at[4 + n]) for o, n in early.items()]

    def late_half(n, h):
        kind, o = LATE[n]
        return wgu.at[kind, o, half_rows(h, half_k)]

    for n in range(len(LATE)):
        local.append(pltpu.make_async_copy(mine_refs[n], late_half(n, dp), lsem.at[4 + len(early) + n]))
    for n in range(TWINNED):
        local.append(pltpu.make_async_copy(twin_refs[n], late_half(n, 1 - dp),
                                           lsem.at[4 + len(early) + len(LATE) + n]))

    def late_pass(n, h):
        return remote(mine_refs[n], late_half(n, h), lxs.at[n - TWINNED], lxr.at[n - TWINNED], twin)

    for copy in local:
        copy.start()
    group_barrier(dp, z, ty)
    me = z * 4 + ty

    def o_copy(n, zt, tt):
        return remote(op_ref.at[zt * 4 + tt], orecv.at[me], os_.at[n], or_.at[n], (dp, zt, tt))

    for n, zt, tt in others(z, ty):
        o_copy(n, zt, tt).start()
    for n in range(TWINNED, len(LATE)):
        late_pass(n, dp).start()
    orecv[me] = op_ref[me]

    def piece(kind, o, h):
        target = lax.rem(z + o, NZ)
        if kind < 2:
            size = half_k // 2
            start = h * half_k + kind * size
            return (wd_ref.at[pl.ds(pl.multiple_of(target * width + start, 16), size)],
                    wdo.at[o, pl.ds(pl.multiple_of(start, 16), size)])
        return (wo_ref.at[pl.ds(pl.multiple_of((target * 2 + h) * head, 16), head)],
                wdo.at[o, pl.ds(pl.multiple_of(width + h * head, 16), head)])

    def w_copy(kind, o):
        src, dst = piece(kind, o, dp)
        return remote(src, dst, ws.at[kind, o], wr.at[kind, o], (dp, lax.rem(z + o, NZ), ty))

    def w_pass(kind, o, h):
        part = piece(kind, o, h)[1]
        return remote(part, part, xs.at[kind, o], xr.at[kind, o], twin)

    slots = (jnp.where(inner, 2, jnp.where(z == 0, 1, 3)), jnp.where(inner, 1, 2),
             jnp.where(z == NZ - 1, 1, 3))
    out_kinds = (2, 0, 1)
    for s in slots:
        for kind in out_kinds:
            w_copy(kind, lax.rem(NZ - s, NZ)).start()

    def pass_on(kind, o):
        w_copy(kind, o).wait_recv()
        w_pass(kind, o, dp).start()

    def project(kind, o):
        wt[...] = wgu[kind, o].T
        acc[kind] += jnp.dot(wt[...], hn_ref[o], preferred_element_type=f32)

    acc[...] = jnp.zeros_like(acc)
    for copy in local:
        copy.wait()

    def project_step(i, carry):
        project(i // NZ, lax.rem(i, NZ))
        return carry

    lax.fori_loop(0, NZ + 1, project_step, 0)
    for n, (kind, o) in enumerate(LATE[1:], 1):
        if n >= TWINNED:
            late_pass(n, 1 - dp).wait_recv()
        lax.fori_loop(kind * NZ + o, kind * NZ + o + 1, project_step, 0)
    for kind in out_kinds:
        pass_on(kind, slots[0])

    def activate(i, carry):
        at = pl.ds(pl.multiple_of(i * 32, 32), 32)
        gate = acc[0, at].astype(bf16).astype(f32)
        up = acc[1, at].astype(bf16).astype(f32)
        lhs[at] = (jax.nn.silu(gate) * up).astype(bf16)
        return carry

    lax.fori_loop(0, width // 32, activate, 0)

    for n, zt, tt in others(z, ty):
        dz, dt = (n + 1) // 4, (n + 1) % 4
        s = source(z, ty, dz, dt)
        remote(op_ref.at[s], orecv.at[s], os_.at[n], or_.at[n], (dp, zt, tt)).wait_recv()
    low = lax.broadcasted_iota(jnp.int32, (head, LANES), 1) < 64
    for b in range(8):
        at = slice(b * LANES, (b + 1) * LANES)
        first, second = swap_halves(orecv[2 * b].astype(f32), orecv[2 * b + 1].astype(f32), low)
        lhs[width:width + head, at] = first.astype(bf16)
        lhs[width + head:width + 2 * head, at] = second.astype(bf16)

    def c_copy(o, yy):
        return remote(parts.at[o, yy * 2 + 1 - c], cbuf.at[o, yy], cs.at[o, yy], cr.at[o, yy], (dp, z, peer_c))

    def y_copy(o):
        return remote(ysend.at[o], yrecv.at[o], ys.at[o], yr.at[o], (dp, z, peer_y))

    def step_of(o):
        return jnp.where(lax.rem(z - o + NZ, NZ) > z, 1, -1)

    def z_copy(o):
        step = step_of(o)
        slot = lax.rem(o + step + NZ, NZ)
        side = (1 - step) // 2
        return remote(zsend.at[o], zrecv.at[side, slot], zs.at[o], zr.at[side, slot], (dp, z + step, ty))

    def z_arrived(o, side):
        return remote(zsend.at[o], zrecv.at[side, o], zs.at[o], zr.at[side, o], (dp, z, peer_y))

    def multiply(o):
        part = dot00(wdo[o], lhs[...]).astype(bf16)
        for t in range(4):
            parts[o, t] = part[t * (width // 4):(t + 1) * (width // 4)]

    def to_core(o):
        c_copy(o, 1 - y).start()
        c_copy(o, y).start()

    def to_y(o):
        c_copy(o, 1 - y).wait_recv()
        ysend[o] = (parts[o, peer_y].astype(f32) + cbuf[o, 1 - y].astype(f32)).astype(bf16)
        y_copy(o).start()

    def pair_sum(o):
        c_copy(o, y).wait_recv()
        y_copy(o).wait_recv()
        return parts[o, ty].astype(f32) + cbuf[o, y].astype(f32) + yrecv[o].astype(f32)

    def to_z(o):
        total = pair_sum(o)
        side = (1 - step_of(o)) // 2

        @pl.when(inner)
        def _():
            z_arrived(o, side).wait_recv()
            zsend[o] = (total + zrecv[side, o].astype(f32)).astype(bf16)

        @pl.when(jnp.logical_not(inner))
        def _():
            zsend[o] = total.astype(bf16)

        z_copy(o).start()

    def slot_of(k):
        return jnp.where(k == 0, 0, jnp.where(k == 1, slots[0], jnp.where(k == 2, slots[1], slots[2])))

    def output_step(k, carry):
        o = slot_of(k)

        @pl.when(jnp.logical_and(k > 0, k < 3))
        def _():
            for kind in out_kinds:
                pass_on(kind, slot_of(k + 1))

        @pl.when(k > 0)
        def _():
            for kind in out_kinds:
                w_pass(kind, o, 1 - dp).wait_recv()

        multiply(o)
        to_core(o)
        pl.when(k > 0)(lambda: to_y(slot_of(k - 1)))
        pl.when(k > 1)(lambda: to_z(slot_of(k - 1)))
        return carry

    lax.fori_loop(0, NZ, output_step, 0)
    to_y(slots[2])
    to_z(slots[2])

    total = pair_sum(0) + res_ref[...].astype(f32)

    @pl.when(z == 0)
    def _():
        z_arrived(0, 1).wait_recv()
        out_ref[...] = (total + zrecv[1, 0].astype(f32)).astype(bf16)

    @pl.when(z == NZ - 1)
    def _():
        z_arrived(0, 0).wait_recv()
        out_ref[...] = (total + zrecv[0, 0].astype(f32)).astype(bf16)

    @pl.when(inner)
    def _():
        z_arrived(0, 0).wait_recv()
        z_arrived(0, 1).wait_recv()
        out_ref[...] = (total + zrecv[0, 0].astype(f32) + zrecv[1, 0].astype(f32)).astype(bf16)

    for kind, o in [(k, o) for k in out_kinds for o in range(1, NZ)]:
        w_copy(kind, o).wait_send()
        w_pass(kind, o, dp).wait_send()
    for n in range(TWINNED, len(LATE)):
        late_pass(n, dp).wait_send()
    for n, zt, tt in others(z, ty):
        o_copy(n, zt, tt).wait_send()
    for o in range(NZ):
        y_copy(o).wait_send()
        for yy in range(2):
            c_copy(o, yy).wait_send()
        if o:
            z_copy(o).wait_send()


def last_stage(hn, packets, mine, twin, gate, w_gate, w_up, w_down, w_out, residual_t):
    _, width, rows = hn.shape
    cols = width // 4
    dma, bf16 = pltpu.SemaphoreType.DMA, jnp.bfloat16
    anywhere, vmem = pl.BlockSpec(memory_space=pl.ANY), pl.BlockSpec(memory_space=pltpu.VMEM)
    buf = lambda *lead: pltpu.VMEM(lead + (cols, rows), bf16)
    return pl.pallas_call(
        last_kernel,
        out_shape=jax.ShapeDtypeStruct((cols, rows), bf16),
        in_specs=[anywhere] * (len(LATE) + TWINNED) + [vmem, vmem] + [anywhere] * 5 + [vmem], out_specs=vmem,
        scratch_shapes=[
            pltpu.VMEM((2, NZ, width, width), bf16), pltpu.VMEM((NZ, width + 160, width), bf16),
            pltpu.VMEM((width, width), bf16), pltpu.VMEM((width + 160, rows), bf16),
            pltpu.VMEM((2, width, rows), jnp.float32), pltpu.VMEM((16, 80, LANES), bf16),
            buf(NZ, 4), buf(NZ, 2), buf(NZ), buf(NZ), buf(NZ), buf(2, NZ),
            dma((4 + len(GATE_EARLY) + len(LATE) + TWINNED,)), dma((15,)), dma((15,)),
            dma((3, NZ)), dma((3, NZ)), dma((3, NZ)), dma((3, NZ)),
            dma((len(LATE) - TWINNED,)), dma((len(LATE) - TWINNED,)),
            dma((NZ, 2)), dma((NZ, 2)), dma((NZ,)), dma((NZ,)), dma((NZ,)), dma((2, NZ))],
        compiler_params=pltpu.CompilerParams(collective_id=1, has_side_effects=True,
                                             vmem_limit_bytes=56 * 2**20),
        name="last_stage",
    )(*mine, *twin, hn, packets, gate, w_gate, w_up, w_down, w_out, residual_t)


def rope_rotate(vectors, positions):
    head_dim = vectors.shape[-1]
    half_dim = head_dim // 2
    inv_freq = ROPE_BASE ** (-2.0 * jnp.arange(half_dim, dtype=jnp.float32) / head_dim)
    angles = positions.astype(jnp.float32)[:, None] * inv_freq[None, :]
    bcast_shape = (angles.shape[0],) + (1,) * (vectors.ndim - 2) + (half_dim,)
    cos_part = jnp.cos(angles).reshape(bcast_shape)
    sin_part = jnp.sin(angles).reshape(bcast_shape)
    vec_f32 = vectors.astype(jnp.float32)
    first_half = vec_f32[..., :half_dim]
    second_half = vec_f32[..., half_dim:]
    rotated = jnp.concatenate([first_half * cos_part - second_half * sin_part, second_half * cos_part + first_half * sin_part], axis=-1)
    return rotated.astype(jnp.bfloat16)


def attend_rows(query_rot, key_rot, value_new, k_cache, v_cache, lengths):
    positions = jnp.arange(k_cache.shape[1], dtype=jnp.int32)
    write_mask = (positions[None, :] == lengths[:, None])[:, :, None]
    k_updated = jnp.where(write_mask, key_rot[:, None, :], k_cache)
    v_updated = jnp.where(write_mask, value_new[:, None, :], v_cache)
    scores = jnp.einsum('rhd,rtd->rht', query_rot, k_updated, preferred_element_type=jnp.float32) * (query_rot.shape[-1] ** -0.5)
    valid_mask = (positions[None, :] <= lengths[:, None])[:, None, :]
    scores = jnp.where(valid_mask, scores, -1e30)
    attn_probs = jax.nn.softmax(scores, axis=-1).astype(jnp.bfloat16)
    attended = jnp.einsum('rht,rtd->rhd', attn_probs, v_updated, preferred_element_type=jnp.float32).astype(jnp.bfloat16)
    return attended, k_updated, v_updated


def solution(mesh):
    row_axes = ('dp', 'tx', 'tyz')

    def decode_layer(residual, ln_scale, w_query, w_key, w_value, w_gate, w_up, w_out, w_down, k_cache, v_cache, lengths):
        rows_all, cols = residual.shape
        rows = k_cache.shape[0]
        head_dim = w_key.shape[1]
        k_slice = w_gate.shape[0]
        ty = lax.axis_index('tyz')
        wq_t = w_query.T.reshape(NZ, 2 * head_dim, k_slice)
        w_kv = jnp.concatenate([w_key.T, w_value.T], axis=0).reshape(NZ, 4, 10, k_slice)
        w_kv = lax.dynamic_index_in_dim(w_kv, ty, 1, keepdims=False)
        wqkv = jnp.concatenate([wq_t, jnp.pad(w_kv, ((0, 0), (0, 6), (0, 0)))], axis=1)
        x_ext = jnp.concatenate([residual.T, jnp.broadcast_to(ln_scale[:, None], (cols, LANES))], axis=1)
        hn, qkv, gate = first_stage(x_ext, wqkv, w_gate, rows_all)

        dp, z = lax.axis_index('dp'), lax.axis_index('tx')
        half_k, width = k_slice // 2, 4 * cols
        gate_late, up_late, qkv = lax.optimization_barrier((w_gate, w_up, qkv))
        mine, twin = [], []
        for kind, o in LATE:
            block = lax.dynamic_slice((gate_late, up_late)[kind], (dp * half_k, lax.rem(z + o, NZ) * width),
                                      (half_k, width))
            n = len(mine)
            mine.append(lax.ppermute(block, 'tx', [(i, (i + o) % NZ) for i in range(NZ)]))
            if n < TWINNED:
                twin.append(lax.ppermute(mine[-1], 'dp', [(0, 1), (1, 0)]))
        query = qkv[:, :head_dim].reshape(16, head_dim, 2, rows).transpose(3, 0, 2, 1).reshape(rows, 32, head_dim)
        kv = lax.dynamic_slice_in_dim(qkv[:, head_dim:head_dim + 10], lax.rem(ty, 2) * rows, rows, axis=2)
        kv = kv.reshape(2 * head_dim, rows).T
        query_rot = rope_rotate(query, lengths)
        key_rot = rope_rotate(kv[:, :head_dim], lengths)
        attended, k_updated, v_updated = attend_rows(query_rot, key_rot, kv[:, head_dim:], k_cache, v_cache, lengths)
        packets = attended.reshape(rows, 16, 2, head_dim).transpose(1, 3, 2, 0).reshape(16, head_dim, 2 * rows)
        new_resid = last_stage(hn, packets, mine, twin, gate, w_gate, w_up, w_down, w_out, residual.T).T
        return new_resid, k_updated, v_updated

    full = P(row_axes)
    res_spec = P('dp', ('tx', 'tyz'))
    return jax.shard_map(
        decode_layer, mesh=mesh,
        in_specs=(res_spec, P(('tx', 'tyz')), P('tx', 'tyz'), P('tx'), P('tx'), P('tx', 'tyz'), P('tx', 'tyz'),
                  P('tyz', 'tx'), P('tyz', 'tx'), full, full, full),
        out_specs=(res_spec, full, full), check_vma=False)
```

time: 515 us -> 254 us (0.49)
  the two profiles are of different devices: /device:TPU:0 before, /device:TPU:24 now
where the time goes in v2:
time: 254 us
  Pallas kernels  174 us (69%)
  other arithmetic  21.7 us (9%)
  waiting for transfers between devices  20.7 us (8%)
  local copies, waits for them, and re-layouts  20.1 us (8%)
  matrix products  11 us (4%)
  starting transfers between devices  5.7 us (2%)
    pallas_call x1, Pallas kernels, last_stage(): pl.pallas_call(last_kernel, out_shape=jax.ShapeDtypeStruct((cols, rows),...  101 us
    pallas_call x1, Pallas kernels, first_stage(): pl.pallas_call(first_kernel, out_shape=(jax.ShapeDtypeStruct((NZ, width,...  72.4 us
    ppermute x4, waiting for transfers between devices, decode_layer(): lax.ppermute(block, 'tx', [(i, (i + o) % NZ) for i in range(NZ)])  20.6 us
    select_n x1, other arithmetic, attend_rows(): k_updated = jnp.where(write_mask, key_rot[:, None, :], k_cache)  13 us
    unnamed x23, local copies, waits for them, and re-layouts  10.5 us
    dot_general x1, matrix products, attend_rows(): jnp.einsum('rht,rtd->rhd', attn_probs, v_updated, preferred_element_type=...  9.35 us
    sub x1, other arithmetic, attend_rows(): attn_probs = jax.nn.softmax(scores, axis=-1).astype(jnp.bfloat16)  5.11 us
  transfers between devices with their start and end apart: 6, of which 3 were waited for; matrix products, arithmetic and copies ran while one was open for 14% of the time, Pallas kernels for 0%

profile of v2, /device:TPU:24, one launch (start us, length us, event | category | flops | bytes accessed | tf_op | source)
XLA Modules:
  0.0 253.7 jit_solution(6783537607257995344)
XLA Ops:
  0.7 1.0 pad_maximum_fusion.1
  1.7 1.8 copy.19
  4.4 1.0 pad_maximum_fusion.x_ref
  5.4 1.9 copy-done
  7.3 72.4 %first_stage.1 = (bf16[4,640,1024]{2,1,0:T(8,128)(2,1)S(1)}, bf16[16,96,128]{2,1,0:T(8,128)(2,1)S(1)}, bf16[2,640,640]{2,1,0:T(8,128)(2,1)S(1)}) custom-call(bf16[160,1152]{1,0:T(8,128)(2,1)S(1)} %pad_maximum_fusion.x_ref, bf16[4,176,640]{2,1,0:T(8,128)(2,1)S(1)} %fusion.8.wqkv_ref, bf16[640,2560]{1,0:T(8,128)(2,1)S(1)} %copy-done), custom_call_target="tpu_custom_call" | custom-call | tf_op jit(solution)/shard_map/first_stage/pallas_call | solution.py:232
  79.8 2.4 copy-done.1
  82.2 1.2 copy-done.2
  83.4 2.3 fusion.16
  85.7 2.4 collective-permute-start.2
  88.1 1.8 dynamic_slice.20
  90.0 2.5 collective-permute-start
  92.5 0.8 iota_compare_fusion.2
  94.3 0.8 copy.21
  95.7 13.0 %broadcast_select_fusion.1 = (bf16[64,1024,80]{1,2,0:T(8,128)(2,1)S(1)}, bf16[64,1024,80]{1,2,0:T(8,128)(2,1)}) fusion(bf16[64,1024,80]{1,2,0:T(8,128)(2,1)} %param.21, pred[64,1024]{1,0:T(8,128)(4,1)S(1)} %get-tuple-element.31, bf16[64,80]{1,0:T(8,128)(2,1)S(1)} %copy.24, bf16[64,1024,80]{1,2,0:T(8,128)(2,1)} %param.22, bf16[64,80]{1,0:T(8,128)(2,1)S(1)} %copy.25), kind=kLoop, calls=%fused_computation.2 | loop fusion | flops 10485760 | bytes 42029056 | tf_op jit(solution)/shard_map/jit(_where)/select_n | solution.py:527
  108.7 1.6 fusion.9
  110.4 2.4 copy-done.3
  112.8 5.1 %fusion.17 = (f32[64,32]{1,0:T(8,128)S(1)}, f32[64,32,1024]{2,1,0:T(8,128)}) fusion(f32[64,32,1024]{2,1,0:T(8,128)S(1)} %fusion.9, pred[64,1024]{1,0:T(8,128)(4,1)S(1)} %copy-done.9), kind=kOutput, calls=%fused_computation.39 | output fusion | flops 12583935 | bytes 16850944 | tf_op jit(solution)/shard_map/sub | solution.py:532
  117.9 3.1 %collective-permute-done.1.refs_1_ = bf16[320,640]{1,0:T(8,128)(2,1)S(1)} collective-permute-done((bf16[320,640]{1,0:T(8,128)(2,1)}, bf16[320,640]{1,0:T(8,128)(2,1)S(1)}, u32[]{:S(2)}, u32[]{:S(2)}) %collective-permute-start.1) | collective-permute-done | bytes 409632 | tf_op jit(solution)/shard_map/ppermute | solution.py:561
  121.0 17.5 %collective-permute-done.refs_0_ = bf16[320,640]{1,0:T(8,128)(2,1)S(1)} collective-permute-done((bf16[320,640]{1,0:T(8,128)(2,1)}, bf16[320,640]{1,0:T(8,128)(2,1)S(1)}, u32[]{:S(2)}, u32[]{:S(2)}) %collective-permute-start) | collective-permute-done | bytes 409632 | tf_op jit(solution)/shard_map/ppermute | solution.py:561
  138.5 0.7 collective-permute-start.4
  139.2 9.4 %fusion.7 = bf16[64,32,80]{2,1,0:T(8,128)(2,1)S(1)} fusion(bf16[64,1024,80]{1,2,0:T(8,128)(2,1)} %get-tuple-element.39, f32[64,32,1024]{2,1,0:T(8,128)} %get-tuple-element.33, f32[64,32]{1,0:T(8,128)S(1)} %get-tuple-element.32), kind=kOutput, calls=%fused_computation.13 | convolution fusion | flops 339902464 | bytes 19210240 | tf_op jit(solution)/shard_map/rht,rtd->rhd/dot_general | solution.py:533
  148.8 0.9 copy.27.refs_7_
  150.8 101.1 %last_stage.1 = bf16[160,1024]{1,0:T(8,128)(2,1)} custom-call(bf16[320,640]{1,0:T(8,128)(2,1)} %copy-done.7, bf16[320,640]{1,0:T(8,128)(2,1)} %copy-done.4, bf16[320,640]{1,0:T(8,128)(2,1)} %copy-done.5, bf16[320,640]{1,0:T(8,128)(2,1)} %copy-done.6, bf16[320,640]{1,0:T(8,128)(2,1)} %collective-permute-done.4.refs_4_, bf16[320,640]{1,0:T(8,128)(2,1)} %copy-done.8, ...), custom_call_target="tpu_custom_call" | custom-call | tf_op jit(solution)/shard_map/last_stage/pallas_call | solution.py:490
  251.9 1.7 copy.29
  (45 shorter events, 3.7 us)
Async XLA Ops:
  0.6 91.8 %copy-start.10 = (s32[64]{0:T(128)S(1)}, s32[64]{0:T(128)}, u32[]{:S(2)}) copy-start(s32[64]{0:T(128)} %param.23) | copy-start | bytes 772
  5.4 1.9 copy-start
  79.8 2.4 copy-start.1
  82.2 1.2 copy-start.2
  85.7 35.3 %collective-permute-start.1 = (bf16[320,640]{1,0:T(8,128)(2,1)}, bf16[320,640]{1,0:T(8,128)(2,1)S(1)}, u32[]{:S(2)}, u32[]{:S(2)}) collective-permute-start(bf16[320,640]{1,0:T(8,128)(2,1)} %get-tuple-element.17), channel_id=1, source_target_pairs={{0,8},{4,12},{8,0},{12,4},{1,9},{5,13},{9,1},{13,5},{2,10},{6,14},... | collective-permute-start | bytes 1228808 | tf_op jit(solution)/shard_map/ppermute | solution.py:561
  85.7 64.0 %collective-permute-start.2 = (bf16[320,640]{1,0:T(8,128)(2,1)}, bf16[320,640]{1,0:T(8,128)(2,1)S(1)}, u32[]{:S(2)}, u32[]{:S(2)}) collective-permute-start(bf16[320,640]{1,0:T(8,128)(2,1)} %get-tuple-element.16), channel_id=1, source_target_pairs={{0,4},{4,8},{8,12},{12,0},{1,5},{5,9},{9,13},{13,1},{2,6},{6,10},{... | collective-permute-start | bytes 1228808 | tf_op jit(solution)/shard_map/ppermute | solution.py:561
  88.1 61.6 %collective-permute-start.3 = (bf16[320,640]{1,0:T(8,128)(2,1)}, bf16[320,640]{1,0:T(8,128)(2,1)S(1)}, u32[]{:S(2)}, u32[]{:S(2)}) collective-permute-start(bf16[320,640]{1,0:T(8,128)(2,1)} %get-tuple-element.15), channel_id=1, source_target_pairs={{0,12},{4,0},{8,4},{12,8},{1,13},{5,1},{9,5},{13,9},{2,14},{6,2},{... | collective-permute-start | bytes 1228808 | tf_op jit(solution)/shard_map/ppermute | solution.py:561
  90.0 48.5 %collective-permute-start = (bf16[320,640]{1,0:T(8,128)(2,1)}, bf16[320,640]{1,0:T(8,128)(2,1)S(1)}, u32[]{:S(2)}, u32[]{:S(2)}) collective-permute-start(bf16[320,640]{1,0:T(8,128)(2,1)} %dynamic_slice.20), channel_id=1, source_target_pairs={{0,8},{4,12},{8,0},{12,4},{1,9},{5,13},{9,1},{13,5},{2,10},{6,14},... | collective-permute-start | bytes 1228808 | tf_op jit(solution)/shard_map/ppermute | solution.py:561
  108.7 4.1 %copy-start.3 = (bf16[64,1024,80]{1,2,0:T(8,128)(2,1)}, bf16[64,1024,80]{1,2,0:T(8,128)(2,1)S(1)}, u32[]{:S(2)}) copy-start(bf16[64,1024,80]{1,2,0:T(8,128)(2,1)S(1)} %get-tuple-element.38) | copy-start | bytes 31457284
  108.7 4.1 %copy-start.9 = (pred[64,1024]{1,0:T(8,128)(4,1)S(1)}, pred[64,1024]{1,0:T(8,128)(4,1)}, u32[]{:S(2)}) copy-start(pred[64,1024]{1,0:T(8,128)(4,1)} %get-tuple-element.30) | copy-start | bytes 196612
  121.0 27.6 %copy-start.4 = (bf16[320,640]{1,0:T(8,128)(2,1)}, bf16[320,640]{1,0:T(8,128)(2,1)S(1)}, u32[]{:S(2)}) copy-start(bf16[320,640]{1,0:T(8,128)(2,1)S(1)} %collective-permute-done.1.refs_1_) | copy-start | bytes 1228804
  121.0 28.8 %collective-permute-start.5 = (bf16[320,640]{1,0:T(8,128)(2,1)S(1)}, bf16[320,640]{1,0:T(8,128)(2,1)S(1)}, u32[]{:S(2)}, u32[]{:S(2)}) collective-permute-start(bf16[320,640]{1,0:T(8,128)(2,1)S(1)} %collective-permute-done.1.refs_1_), channel_id=1, source_target_pairs={{0,16},{16,0},{1,17},{17,1},{2,18},{18,2},{3,19},{19,3},{4,20},{20... | collective-permute-start | bytes 1228808 | tf_op jit(solution)/shard_map/ppermute | solution.py:563
  138.5 10.1 %copy-start.7 = (bf16[320,640]{1,0:T(8,128)(2,1)}, bf16[320,640]{1,0:T(8,128)(2,1)S(1)}, u32[]{:S(2)}) copy-start(bf16[320,640]{1,0:T(8,128)(2,1)S(1)} %collective-permute-done.refs_0_) | copy-start | bytes 1228804
  138.5 11.5 %collective-permute-start.4 = (bf16[320,640]{1,0:T(8,128)(2,1)S(1)}, bf16[320,640]{1,0:T(8,128)(2,1)}, u32[]{:S(2)}, u32[]{:S(2)}) collective-permute-start(bf16[320,640]{1,0:T(8,128)(2,1)S(1)} %collective-permute-done.refs_0_), channel_id=1, source_target_pairs={{0,16},{16,0},{1,17},{17,1},{2,18},{18,2},{3,19},{19,3},{4,20},{20... | collective-permute-start | bytes 1228808 | tf_op jit(solution)/shard_map/ppermute | solution.py:563
  149.7 0.8 copy-start.5
  149.7 0.9 copy-start.6
  149.8 1.0 copy-start.8

commit v3 on v2

--- a/solution.py
+++ b/solution.py
@@ -57,22 +57,28 @@
 
 GATE_EARLY = (1, 3)
 LATE = ((0, 2), (1, 2), (1, 1), (1, 3))
-TWINNED = 2
-
-
-def first_kernel(x_ref, wqkv_ref, wg_ref, hn_ref, qkv_ref, gate_ref,
-                 gat, wq, q32, packets, lsem, zs, zr, ys, yr, cs, cr,
+TWINNED = 1
+
+
+def first_kernel(x_ref, scale_ref, wq_ref, wkv_ref, wg_ref, hn_out, qkv_ref, gate_ref,
+                 gat, sgat, hn_ref, wqn, wqt, wq, q32, packets, lsem, ss, sr, zs, zr, ys, yr, cs, cr,
                  qs, qr, qxs, qxr, gs, gr, gxs, gxr, as_, ar):
     dp, z, ty = position()
     y, c = ty // 2, lax.rem(ty, 2)
     peer_y, peer_c, twin = (1 - y) * 2 + c, y * 2 + 1 - c, (1 - dp, z, ty)
     f32, bf16 = jnp.float32, jnp.bfloat16
-    cols, rows = x_ref.shape[0], hn_ref.shape[2]
+    cols, rows = x_ref.shape
     width = 4 * cols
     local_x = pltpu.make_async_copy(x_ref, gat.at[0, ty], lsem.at[0])
-    local_w = pltpu.make_async_copy(wqkv_ref.at[z], wq.at[:, pl.ds(0, width)], lsem.at[1])
-    local_x.start()
-    local_w.start()
+    local_w = pltpu.make_async_copy(wq_ref, wqn, lsem.at[1])
+    head = 80
+
+    def kv_rows(target):
+        return pl.ds(pl.multiple_of(jnp.minimum(target * 4 + ty, 9) * 16, 16), 16)
+
+    local_kv = pltpu.make_async_copy(wkv_ref.at[kv_rows(z)], wq.at[pl.ds(2 * head, 16), pl.ds(0, width)], lsem.at[2])
+    for copy in (local_x, local_w, local_kv):
+        copy.start()
     group_barrier(dp, z, ty)
 
     def z_copy(o, step):
@@ -88,16 +94,15 @@
     def c_copy(o, yy, core=c):
         t = yy * 2 + core
         return remote(gat.at[o, t], gat.at[o, t], cs.at[o, yy], cr.at[o, yy], (dp, z, peer_c))
-
-    head = 80
 
     def q_copy(o):
         target = lax.rem(z + o, NZ)
         mine = half_rows(dp, head)
         to = (dp, target, ty)
         at = pl.ds(o * width, width)
-        return (remote(wqkv_ref.at[target, mine], wq.at[mine, at], qs.at[o, 0], qr.at[o, 0], to),
-                remote(wqkv_ref.at[target, pl.ds(2 * head, 16)], wq.at[pl.ds(2 * head, 16), at],
+        rows_ = pl.ds(pl.multiple_of(target * 2 * head + dp * head, 16), head)
+        return (remote(wqt.at[rows_], wq.at[mine, at], qs.at[o, 0], qr.at[o, 0], to),
+                remote(wkv_ref.at[kv_rows(target)], wq.at[pl.ds(2 * head, 16), at],
                        qs.at[o, 1], qr.at[o, 1], to))
 
     def q_pass(o, h):
@@ -121,6 +126,18 @@
     pl.when(z > 0)(lambda: z_copy(0, -1).start())
     y_copy(0).start()
     c_copy(0, y).start()
+
+    def s_copy(n, zt, tt):
+        dz = (n + 1) // 4
+        return remote(scale_ref, sgat.at[dz, ty], ss.at[n], sr.at[n], (dp, zt, tt))
+
+    for n, zt, tt in others(z, ty):
+        s_copy(n, zt, tt).start()
+    local_s = pltpu.make_async_copy(scale_ref, sgat.at[0, ty], lsem.at[3])
+    local_s.start()
+    local_w.wait()
+    wqt[...] = wqn[...].T
+    wq[0:2 * head, 0:width] = wqt[pl.ds(pl.multiple_of(z * 2 * head, 16), 2 * head)]
     for d in range(1, NZ):
         for o, here, onward, step in (
                 (d, z >= d, z < NZ - 1, 1), (NZ - d, z + d < NZ, z > 0, -1)):
@@ -157,16 +174,22 @@
         return v.reshape(v.shape[0] // 8, 8, v.shape[1]).sum(axis=0)
 
     def block(i):
-        return gat[i // 4, lax.rem(i, 4), :, pl.ds(0, rows)].astype(f32)
+        return gat[i // 4, lax.rem(i, 4)].astype(f32)
 
     total = lax.fori_loop(0, 16, lambda i, s: s + fold(block(i)), jnp.zeros((8, rows), f32))
     mean = jnp.sum(total, axis=0, keepdims=True) / (16 * cols)
     total = lax.fori_loop(0, 16, lambda i, s: s + fold(jnp.square(block(i) - mean)), jnp.zeros((8, rows), f32))
     rstd = lax.rsqrt(jnp.sum(total, axis=0, keepdims=True) / (16 * cols) + LN_EPS)
 
+    local_s.wait()
+    for n, zt, tt in others(z, ty):
+        dz, dt = (n + 1) // 4, (n + 1) % 4
+        remote(scale_ref, sgat.at[dz, lax.rem(ty + 4 - dt, 4)], ss.at[n], sr.at[n], (dp, zt, tt)).wait_recv()
+    ones = (lax.broadcasted_iota(jnp.int32, (16, LANES), 0) == 0).astype(f32).astype(bf16)
+
     def normalize(i, carry):
         o, t = i // 4, lax.rem(i, 4)
-        scale = gat[o, t, :, pl.ds(rows, LANES)].astype(f32)
+        scale = dot00(sgat[o, t], ones)[:cols]
         for k in range(rows // LANES):
             at = slice(k * LANES, (k + 1) * LANES)
             v = gat[o, t, :, at].astype(f32)
@@ -175,8 +198,10 @@
         return carry
 
     lax.fori_loop(0, 16, normalize, 0)
-
-    local_w.wait()
+    hn_copy = pltpu.make_async_copy(hn_ref, hn_out, lsem.at[4])
+    hn_copy.start()
+
+    local_kv.wait()
     for o in (2, 1, 3):
         q_copy(o)[1].wait_recv()
         q_pass(o, 1 - dp).wait_recv()
@@ -210,8 +235,10 @@
         g_pass(n, 1 - dp).wait_recv()
         g_pass(n, dp).wait_send()
         g_copy(n, o).wait_send()
+    hn_copy.wait()
     for n, zt, tt in others(z, ty):
         a_copy(n, zt, tt).wait_send()
+        s_copy(n, zt, tt).wait_send()
     for o in range(1, NZ):
         for copy in q_copy(o):
             copy.wait_send()
@@ -223,36 +250,39 @@
         pl.when(jnp.logical_and(z + d < NZ, z > 0))(lambda d=d: z_copy(NZ - d, -1).wait_send())
 
 
-def first_stage(x_ext, wqkv, w_gate, rows):
-    cols = x_ext.shape[0]
+def first_stage(x, scale, w_query_nat, w_kv, w_gate):
+    cols, rows = x.shape
     width = 4 * cols
     dma, bf16 = pltpu.SemaphoreType.DMA, jnp.bfloat16
     early = len(GATE_EARLY)
     anywhere, vmem = pl.BlockSpec(memory_space=pl.ANY), pl.BlockSpec(memory_space=pltpu.VMEM)
+    hbm = pl.BlockSpec(memory_space=pltpu.HBM)
     return pl.pallas_call(
         first_kernel,
         out_shape=(jax.ShapeDtypeStruct((NZ, width, rows), bf16),
                    jax.ShapeDtypeStruct((16, 96, LANES), bf16),
                    jax.ShapeDtypeStruct((early, width, width), bf16)),
-        in_specs=[anywhere] * 3,
-        out_specs=(vmem, vmem, anywhere),
+        in_specs=[hbm] * 5,
+        out_specs=(hbm, vmem, hbm),
         scratch_shapes=[
-            pltpu.VMEM((NZ, 4) + x_ext.shape, bf16), pltpu.VMEM((176, NZ * width), bf16),
+            pltpu.VMEM((NZ, 4, cols, rows), bf16), pltpu.VMEM((NZ, 4, 16, 256), bf16),
+            pltpu.VMEM((NZ, width, rows), bf16), pltpu.VMEM((width, width), bf16),
+            pltpu.VMEM((width, width), bf16), pltpu.VMEM((176, NZ * width), bf16),
             pltpu.VMEM((176, rows), jnp.float32), pltpu.VMEM((16, 96, LANES), bf16),
-            dma((2,)), dma((NZ, 2)), dma((NZ,)), dma((NZ,)), dma((NZ,)), dma((NZ, 2)), dma((NZ, 2)),
+            dma((5,)), dma((15,)), dma((15,)), dma((NZ, 2)), dma((NZ,)), dma((NZ,)), dma((NZ,)), dma((NZ, 2)), dma((NZ, 2)),
             dma((NZ, 2)), dma((NZ, 2)), dma((NZ,)), dma((NZ,)),
             dma((early,)), dma((early,)), dma((early,)), dma((early,)), dma((15,)), dma((15,))],
         compiler_params=pltpu.CompilerParams(collective_id=0, has_side_effects=True,
-                                             vmem_limit_bytes=32 * 2**20),
+                                             vmem_limit_bytes=60 * 2**20),
         name="first_stage",
-    )(x_ext, wqkv, w_gate)
+    )(x, scale, w_query_nat, w_kv, w_gate)
 
 
 def last_kernel(*refs):
     mine_refs, refs = refs[:len(LATE)], refs[len(LATE):]
     twin_refs, refs = refs[:TWINNED], refs[TWINNED:]
-    (hn_ref, op_ref, gate_ref, wg_ref, wu_ref, wd_ref, wo_ref, res_ref, out_ref,
-                wgu, wdo, wt, lhs, acc, orecv, parts, cbuf, ysend, yrecv, zsend, zrecv,
+    (hn_in, op_ref, gate_ref, wg_ref, wu_ref, wd_ref, wo_ref, res_ref, out_ref,
+                hn_ref, wgu, wdo, wt, lhs, acc, orecv, parts, cbuf, ysend, yrecv, zsend, zrecv,
                 lsem, os_, or_, ws, wr, xs, xr, lxs, lxr, cs, cr, ys, yr, zs, zr) = refs
     dp, z, ty = position()
     y, c = ty // 2, lax.rem(ty, 2)
@@ -271,18 +301,19 @@
              pltpu.make_async_copy(wd_ref.at[pl.ds(pl.multiple_of(z * width, 16), width)],
                                    wdo.at[0, pl.ds(0, width)], lsem.at[2]),
              pltpu.make_async_copy(wo_ref.at[pl.ds(pl.multiple_of(z * 2 * head, 16), 2 * head)],
-                                   wdo.at[0, pl.ds(width, 2 * head)], lsem.at[3])]
-    local += [pltpu.make_async_copy(gate_ref.at[n], wgu.at[0, o], lsem.at[4 + n]) for o, n in early.items()]
+                                   wdo.at[0, pl.ds(width, 2 * head)], lsem.at[3]),
+             pltpu.make_async_copy(hn_in, hn_ref, lsem.at[4])]
+    local += [pltpu.make_async_copy(gate_ref.at[n], wgu.at[0, o], lsem.at[5 + n]) for o, n in early.items()]
 
     def late_half(n, h):
         kind, o = LATE[n]
         return wgu.at[kind, o, half_rows(h, half_k)]
 
     for n in range(len(LATE)):
-        local.append(pltpu.make_async_copy(mine_refs[n], late_half(n, dp), lsem.at[4 + len(early) + n]))
+        local.append(pltpu.make_async_copy(mine_refs[n], late_half(n, dp), lsem.at[5 + len(early) + n]))
     for n in range(TWINNED):
         local.append(pltpu.make_async_copy(twin_refs[n], late_half(n, 1 - dp),
-                                           lsem.at[4 + len(early) + len(LATE) + n]))
+                                           lsem.at[5 + len(early) + len(LATE) + n]))
 
     def late_pass(n, h):
         return remote(mine_refs[n], late_half(n, h), lxs.at[n - TWINNED], lxr.at[n - TWINNED], twin)
@@ -344,11 +375,12 @@
 
     lax.fori_loop(0, NZ + 1, project_step, 0)
     for n, (kind, o) in enumerate(LATE[1:], 1):
+        if n == len(LATE) - 1:
+            for k in out_kinds:
+                pass_on(k, slots[0])
         if n >= TWINNED:
             late_pass(n, 1 - dp).wait_recv()
         lax.fori_loop(kind * NZ + o, kind * NZ + o + 1, project_step, 0)
-    for kind in out_kinds:
-        pass_on(kind, slots[0])
 
     def activate(i, carry):
         at = pl.ds(pl.multiple_of(i * 32, 32), 32)
@@ -490,18 +522,18 @@
     return pl.pallas_call(
         last_kernel,
         out_shape=jax.ShapeDtypeStruct((cols, rows), bf16),
-        in_specs=[anywhere] * (len(LATE) + TWINNED) + [vmem, vmem] + [anywhere] * 5 + [vmem], out_specs=vmem,
+        in_specs=[anywhere] * (len(LATE) + TWINNED) + [pl.BlockSpec(memory_space=pltpu.HBM), vmem] + [anywhere] * 5 + [vmem], out_specs=vmem,
         scratch_shapes=[
-            pltpu.VMEM((2, NZ, width, width), bf16), pltpu.VMEM((NZ, width + 160, width), bf16),
+            pltpu.VMEM(hn.shape, bf16), pltpu.VMEM((2, NZ, width, width), bf16), pltpu.VMEM((NZ, width + 160, width), bf16),
             pltpu.VMEM((width, width), bf16), pltpu.VMEM((width + 160, rows), bf16),
             pltpu.VMEM((2, width, rows), jnp.float32), pltpu.VMEM((16, 80, LANES), bf16),
             buf(NZ, 4), buf(NZ, 2), buf(NZ), buf(NZ), buf(NZ), buf(2, NZ),
-            dma((4 + len(GATE_EARLY) + len(LATE) + TWINNED,)), dma((15,)), dma((15,)),
+            dma((5 + len(GATE_EARLY) + len(LATE) + TWINNED,)), dma((15,)), dma((15,)),
             dma((3, NZ)), dma((3, NZ)), dma((3, NZ)), dma((3, NZ)),
             dma((len(LATE) - TWINNED,)), dma((len(LATE) - TWINNED,)),
             dma((NZ, 2)), dma((NZ, 2)), dma((NZ,)), dma((NZ,)), dma((NZ,)), dma((2, NZ))],
         compiler_params=pltpu.CompilerParams(collective_id=1, has_side_effects=True,
-                                             vmem_limit_bytes=56 * 2**20),
+                                             vmem_limit_bytes=60 * 2**20),
         name="last_stage",
     )(*mine, *twin, hn, packets, gate, w_gate, w_up, w_down, w_out, residual_t)
 
@@ -538,17 +570,14 @@
     row_axes = ('dp', 'tx', 'tyz')
 
     def decode_layer(residual, ln_scale, w_query, w_key, w_value, w_gate, w_up, w_out, w_down, k_cache, v_cache, lengths):
-        rows_all, cols = residual.shape
+        _, cols = residual.shape
         rows = k_cache.shape[0]
         head_dim = w_key.shape[1]
         k_slice = w_gate.shape[0]
         ty = lax.axis_index('tyz')
-        wq_t = w_query.T.reshape(NZ, 2 * head_dim, k_slice)
-        w_kv = jnp.concatenate([w_key.T, w_value.T], axis=0).reshape(NZ, 4, 10, k_slice)
-        w_kv = lax.dynamic_index_in_dim(w_kv, ty, 1, keepdims=False)
-        wqkv = jnp.concatenate([wq_t, jnp.pad(w_kv, ((0, 0), (0, 6), (0, 0)))], axis=1)
-        x_ext = jnp.concatenate([residual.T, jnp.broadcast_to(ln_scale[:, None], (cols, LANES))], axis=1)
-        hn, qkv, gate = first_stage(x_ext, wqkv, w_gate, rows_all)
+        w_kv = jnp.concatenate([w_key.T, w_value.T], axis=0)
+        scale = jnp.pad(jnp.broadcast_to(ln_scale[None, :], (16, cols)), ((0, 0), (0, 256 - cols)))
+        hn, qkv, gate = first_stage(residual.T, scale, w_query, w_kv, w_gate)
 
         dp, z = lax.axis_index('dp'), lax.axis_index('tx')
         half_k, width = k_slice // 2, 4 * cols
@@ -562,7 +591,7 @@
             if n < TWINNED:
                 twin.append(lax.ppermute(mine[-1], 'dp', [(0, 1), (1, 0)]))
         query = qkv[:, :head_dim].reshape(16, head_dim, 2, rows).transpose(3, 0, 2, 1).reshape(rows, 32, head_dim)
-        kv = lax.dynamic_slice_in_dim(qkv[:, head_dim:head_dim + 10], lax.rem(ty, 2) * rows, rows, axis=2)
+        kv = lax.dynamic_slice_in_dim(qkv[:10, head_dim:], lax.rem(ty, 2) * rows, rows, axis=2)
         kv = kv.reshape(2 * head_dim, rows).T
         query_rot = rope_rotate(query, lengths)
         key_rot = rope_rotate(kv[:, :head_dim], lengths)

time: 254 us -> 245 us (0.965)
  local copies, waits for them, and re-layouts: 20.1 us -> 12.1 us
    unnamed x23 -> x9, local copies, waits for them, and re-layouts: 10.5 us -> 4.9 us
  transfers between devices with their start and end apart: 6 -> 5, of which waited for: 3 -> 2; matrix products, arithmetic and copies ran while one was open for 14% -> 15% of each run, Pallas kernels for 0% -> 0%
where the time goes in v3:
time: 245 us
  Pallas kernels  172 us (70%)
  other arithmetic  22.3 us (9%)
  waiting for transfers between devices  20.5 us (8%)
  local copies, waits for them, and re-layouts  12.1 us (5%)
  matrix products  11 us (4%)
  starting transfers between devices  5.61 us (2%)
    pallas_call x1, Pallas kernels, last_stage(): pl.pallas_call(last_kernel, out_shape=jax.ShapeDtypeStruct((cols, rows),...  99.6 us
    pallas_call x1, Pallas kernels, first_stage(): pl.pallas_call(first_kernel, out_shape=(jax.ShapeDtypeStruct((NZ, width,...  72.7 us
    ppermute x4, waiting for transfers between devices, decode_layer(): lax.ppermute(block, 'tx', [(i, (i + o) % NZ) for i in range(NZ)])  20 us
    select_n x1, other arithmetic, attend_rows(): k_updated = jnp.where(write_mask, key_rot[:, None, :], k_cache)  13.1 us
    dot_general x1, matrix products, attend_rows(): jnp.einsum('rht,rtd->rhd', attn_probs, v_updated, preferred_element_type=...  9.37 us
    sub x1, other arithmetic, attend_rows(): attn_probs = jax.nn.softmax(scores, axis=-1).astype(jnp.bfloat16)  5.1 us
    ppermute x4, starting transfers between devices, decode_layer(): lax.ppermute(block, 'tx', [(i, (i + o) % NZ) for i in range(NZ)])  5.07 us
  transfers between devices with their start and end apart: 5, of which 2 were waited for; matrix products, arithmetic and copies ran while one was open for 15% of the time, Pallas kernels for 0%

profile of v3, /device:TPU:24, one launch (start us, length us, event | category | flops | bytes accessed | tf_op | source)
XLA Modules:
  0.0 244.6 jit_solution(13659847579724230361)
XLA Ops:
  0.7 1.6 pad_maximum_fusion.wkv_ref
  2.3 0.7 pad.6
  3.0 0.6 pad.7.scale_ref
  3.6 72.7 %first_stage.1 = (bf16[4,640,1024]{2,1,0:T(8,128)(2,1)}, bf16[16,96,128]{2,1,0:T(8,128)(2,1)}, bf16[2,640,640]{2,1,0:T(8,128)(2,1)}) custom-call(bf16[160,1024]{1,0:T(8,128)(2,1)} %bitcast.20, bf16[16,256]{1,0:T(8,128)(2,1)} %pad.7.scale_ref, bf16[640,640]{1,0:T(8,128)(2,1)} %wq_ref.1, bf16[160,640]{1,0:T(8,128)(2,1)} %pad_maximum_fusion.wkv_ref, ...), custom_call_target="tpu_custom_call" | custom-call | tf_op jit(solution)/shard_map/first_stage/pallas_call | solution.py:260
  76.3 1.4 fusion.14
  77.8 2.4 collective-permute-start.2
  80.2 1.0 dynamic_slice.15
  81.2 2.6 %collective-permute-start = (bf16[320,640]{1,0:T(8,128)(2,1)S(1)}, bf16[320,640]{1,0:T(8,128)(2,1)}, u32[]{:S(2)}, u32[]{:S(2)}) collective-permute-start(bf16[320,640]{1,0:T(8,128)(2,1)S(1)} %dynamic_slice.15), channel_id=1, source_target_pairs={{0,8},{4,12},{8,0},{12,4},{1,9},{5,13},{9,1},{13,5},{2,10},{6,14},... | collective-permute-start | bytes 1228808 | tf_op jit(solution)/shard_map/ppermute | solution.py:590
  83.8 0.8 iota_compare_fusion.1
  84.6 0.8 slice.27
  85.4 1.0 slice_convert_fusion
  87.4 0.8 copy.18
  88.2 0.5 subtract_convert_fusion
  88.8 13.1 %broadcast_select_fusion.1 = (bf16[64,1024,80]{1,2,0:T(8,128)(2,1)S(1)}, bf16[64,1024,80]{1,2,0:T(8,128)(2,1)}) fusion(bf16[64,1024,80]{1,2,0:T(8,128)(2,1)} %param.21, pred[64,1024]{1,0:T(8,128)(4,1)S(1)} %get-tuple-element.31, bf16[64,80]{1,0:T(8,128)(2,1)S(1)} %copy.21, bf16[64,1024,80]{1,2,0:T(8,128)(2,1)} %param.22, bf16[64,80]{1,0:T(8,128)(2,1)S(1)} %copy.22), kind=kLoop, calls=%fused_computation.2 | loop fusion | flops 10485760 | bytes 42029056 | tf_op jit(solution)/shard_map/jit(_where)/select_n | solution.py:559
  101.9 1.7 fusion.7
  103.5 2.4 copy-done
  105.9 5.1 %fusion.15 = (f32[64,32]{1,0:T(8,128)S(1)}, f32[64,32,1024]{2,1,0:T(8,128)}) fusion(f32[64,32,1024]{2,1,0:T(8,128)S(1)} %fusion.7, pred[64,1024]{1,0:T(8,128)(4,1)S(1)} %copy-done.2), kind=kOutput, calls=%fused_computation.34 | output fusion | flops 12583935 | bytes 16850944 | tf_op jit(solution)/shard_map/sub | solution.py:564
  111.0 20.0 %collective-permute-done.refs_0_ = bf16[320,640]{1,0:T(8,128)(2,1)} collective-permute-done((bf16[320,640]{1,0:T(8,128)(2,1)S(1)}, bf16[320,640]{1,0:T(8,128)(2,1)}, u32[]{:S(2)}, u32[]{:S(2)}) %collective-permute-start) | collective-permute-done | bytes 409632 | tf_op jit(solution)/shard_map/ppermute | solution.py:590
  131.0 0.5 collective-permute-start.4
  131.5 9.4 %fusion.6 = bf16[64,32,80]{2,1,0:T(8,128)(2,1)S(1)} fusion(bf16[64,1024,80]{1,2,0:T(8,128)(2,1)} %get-tuple-element.39, f32[64,32,1024]{2,1,0:T(8,128)} %get-tuple-element.33, f32[64,32]{1,0:T(8,128)S(1)} %get-tuple-element.32), kind=kOutput, calls=%fused_computation.11 | convolution fusion | flops 339902464 | bytes 19210240 | tf_op jit(solution)/shard_map/rht,rtd->rhd/dot_general | solution.py:565
  141.1 0.9 copy.24.refs_6_
  142.6 0.7 copy-done.1
  143.3 99.6 %last_stage.1 = bf16[160,1024]{1,0:T(8,128)(2,1)} custom-call(bf16[320,640]{1,0:T(8,128)(2,1)} %collective-permute-done.refs_0_, bf16[320,640]{1,0:T(8,128)(2,1)} %collective-permute-done.1.refs_1_, bf16[320,640]{1,0:T(8,128)(2,1)} %collective-permute-done.2.refs_2_, bf16[320,640]{1,0:T(8,128)(2,1)} %collective-permute-done.3.refs_3_, ...), custom_call_target="tpu_custom_call" | custom-call | tf_op jit(solution)/shard_map/last_stage/pallas_call | solution.py:522
  242.9 1.7 copy.26
  (24 shorter events, 1.8 us)
Async XLA Ops:
  0.6 83.2 %copy-start.3 = (s32[64]{0:T(128)S(1)}, s32[64]{0:T(128)}, u32[]{:S(2)}) copy-start(s32[64]{0:T(128)} %param.23) | copy-start | bytes 772
  77.7 64.4 %collective-permute-start.1 = (bf16[320,640]{1,0:T(8,128)(2,1)S(1)}, bf16[320,640]{1,0:T(8,128)(2,1)}, u32[]{:S(2)}, u32[]{:S(2)}) collective-permute-start(bf16[320,640]{1,0:T(8,128)(2,1)S(1)} %get-tuple-element.17), channel_id=1, source_target_pairs={{0,8},{4,12},{8,0},{12,4},{1,9},{5,13},{9,1},{13,5},{2,10},{6,14},... | collective-permute-start | bytes 1228808 | tf_op jit(solution)/shard_map/ppermute | solution.py:590
  77.8 64.3 %collective-permute-start.2 = (bf16[320,640]{1,0:T(8,128)(2,1)S(1)}, bf16[320,640]{1,0:T(8,128)(2,1)}, u32[]{:S(2)}, u32[]{:S(2)}) collective-permute-start(bf16[320,640]{1,0:T(8,128)(2,1)S(1)} %get-tuple-element.16), channel_id=1, source_target_pairs={{0,4},{4,8},{8,12},{12,0},{1,5},{5,9},{9,13},{13,1},{2,6},{6,10},{... | collective-permute-start | bytes 1228808 | tf_op jit(solution)/shard_map/ppermute | solution.py:590
  80.2 61.9 %collective-permute-start.3 = (bf16[320,640]{1,0:T(8,128)(2,1)S(1)}, bf16[320,640]{1,0:T(8,128)(2,1)}, u32[]{:S(2)}, u32[]{:S(2)}) collective-permute-start(bf16[320,640]{1,0:T(8,128)(2,1)S(1)} %get-tuple-element.15), channel_id=1, source_target_pairs={{0,12},{4,0},{8,4},{12,8},{1,13},{5,1},{9,5},{13,9},{2,14},{6,2},{... | collective-permute-start | bytes 1228808 | tf_op jit(solution)/shard_map/ppermute | solution.py:590
  81.2 49.8 %collective-permute-start = (bf16[320,640]{1,0:T(8,128)(2,1)S(1)}, bf16[320,640]{1,0:T(8,128)(2,1)}, u32[]{:S(2)}, u32[]{:S(2)}) collective-permute-start(bf16[320,640]{1,0:T(8,128)(2,1)S(1)} %dynamic_slice.15), channel_id=1, source_target_pairs={{0,8},{4,12},{8,0},{12,4},{1,9},{5,13},{9,1},{13,5},{2,10},{6,14},... | collective-permute-start | bytes 1228808 | tf_op jit(solution)/shard_map/ppermute | solution.py:590
  101.8 4.1 %copy-start = (bf16[64,1024,80]{1,2,0:T(8,128)(2,1)}, bf16[64,1024,80]{1,2,0:T(8,128)(2,1)S(1)}, u32[]{:S(2)}) copy-start(bf16[64,1024,80]{1,2,0:T(8,128)(2,1)S(1)} %get-tuple-element.38) | copy-start | bytes 31457284
  101.9 4.1 %copy-start.2 = (pred[64,1024]{1,0:T(8,128)(4,1)S(1)}, pred[64,1024]{1,0:T(8,128)(4,1)}, u32[]{:S(2)}) copy-start(pred[64,1024]{1,0:T(8,128)(4,1)} %get-tuple-element.30) | copy-start | bytes 196612
  131.0 11.6 %collective-permute-start.4 = (bf16[320,640]{1,0:T(8,128)(2,1)}, bf16[320,640]{1,0:T(8,128)(2,1)S(1)}, u32[]{:S(2)}, u32[]{:S(2)}) collective-permute-start(bf16[320,640]{1,0:T(8,128)(2,1)} %collective-permute-done.refs_0_), channel_id=1, source_target_pairs={{0,16},{16,0},{1,17},{17,1},{2,18},{18,2},{3,19},{19,3},{4,20},{20... | collective-permute-start | bytes 1228808 | tf_op jit(solution)/shard_map/ppermute | solution.py:592
  142.6 0.7 copy-start.1
